TPU v7x, 512 devices: a whole 4x8x8 slice. The times are simulated.
512 devices in a mesh: dp: 32 (over x, z), patch: 16 (over y, core).
Axes of the slice: x: 4, y: 8, z: 8, core: 2. Of those that a mesh axis runs over, the one named last changes fastest.
Arguments:
- query_rows: bfloat16 [32, 2048, 576], P('dp', 'patch'), may hold values from -6 to 6
- key_rows: bfloat16 [32, 2048, 576], P('dp', 'patch'), may hold values from -6 to 6
- value_rows: bfloat16 [32, 2048, 576], P('dp', 'patch'), may hold values from -6 to 6
- out_weight: bfloat16 [576, 1152], replicated, may hold values from -0.25 to 0.25
- target: bfloat16 [32, 2048, 1152], P('dp', 'patch'), may hold values from -6 to 6
- lengths: int32 [32], P('dp'), may hold values from 256 to 2048
- segments: int32 [32, 2048], P('dp', 'patch'), may hold values from 0 to 7, never falling along the last dimension, each value on 1 to 1024 neighbouring positions
Outputs:
- query_grad: float32 [32, 2048, 576], P('dp', 'patch')
- key_grad: float32 [32, 2048, 576], P('dp', 'patch')
- value_grad: float32 [32, 2048, 576], P('dp', 'patch')
- weight_grad: float32 [576, 1152], P('patch', 'dp')
- loss: float32 [], replicated
All inputs are finite; a program needn't handle non-finite values.
Results may differ from a plain program's by a relative error of at most 0.024.
Values may be sent and summed in bfloat16 or wider, within the bound.
A program may use at most 64 MiB of HBM per device.

v0:
```python
import math

import jax
import jax.numpy as jnp
from jax import lax
from jax.sharding import Mesh
from jax.sharding import PartitionSpec as P

WIDTH = 1152
HEADS = 8
HEAD_DIM = 72
FEAT = 576
PATCH = ("patch_0", "patch_1")
DP = ("dp_0", "dp_1")
DP_PATCH = ("dp_0", "dp_1", "patch_0", "patch_1")


NEG_LARGE = -1e30


def from_everyone(value, axis):
    copies = jnp.broadcast_to(value, (lax.axis_size(axis), *value.shape))
    return lax.all_to_all(copies, axis, split_axis=0, concat_axis=0, tiled=True)


def of_everyone(value, axis):
    return from_everyone(value, axis).sum(axis=0)


def sent_together(arrays, axis, dim, along):
    ends, at = ([], 0)
    for a in arrays[:-1]:
        at += a.shape[along]
        ends.append(at)
    both = jnp.concatenate(arrays, axis=along)
    return tuple(jnp.split(lax.all_gather(both, axis, axis=dim, tiled=True), ends, axis=along))


def by_axis(value, axes):
    for axis in axes:
        value = lax.psum(value, axis)
    return value


def in_blocks(value, dim, peers):
    shape = value.shape
    pieces = value.reshape(*shape[:dim], peers, shape[dim] // peers, *shape[dim + 1 :])
    return jnp.moveaxis(pieces, dim, 0)


def sum_at_owner(value, axis, dim):
    peers = lax.axis_size(axis)
    pieces = lax.all_to_all(in_blocks(value, dim, peers), axis, 0, 0, tiled=True)
    return jnp.sum(pieces.astype(jnp.float32), axis=0)


def head_view(rows):
    return rows.reshape(rows.shape[0], HEADS, HEAD_DIM)


def pair_mask(query_group, key_group):
    return (query_group[:, None] == key_group[None, :])[None, :, :]


def forward_block(running, query_heads, own_group, group_all, pieces):
    run_max, run_denom, run_accum = running
    score_scale = 1.0 / math.sqrt(HEAD_DIM)
    key_heads = head_view(pieces[0][0])
    value_heads = head_view(pieces[1][0])
    allowed = pair_mask(own_group, group_all)
    scores = (
        jnp.einsum("qhe,khe->hqk", query_heads, key_heads, preferred_element_type=jnp.float32)
        * score_scale
    )
    masked = jnp.where(allowed, scores, NEG_LARGE)
    new_max = jnp.maximum(run_max, jnp.max(masked, axis=2))
    probs = jnp.where(allowed, jnp.exp(masked - new_max[:, :, None]), 0.0)
    shrink = jnp.exp(run_max - new_max)
    run_denom = jnp.sum(probs, axis=2)
    added = jnp.einsum(
        "hqk,khe->qhe", probs.astype(jnp.bfloat16), value_heads, preferred_element_type=jnp.float32
    )
    run_accum = run_accum * shrink.T[:, :, None] + added
    return (new_max, run_denom, run_accum)


def query_grad_block(query_heads, grad_heads, log_norm, delta, own_group, group_all, pieces):
    score_scale = 1.0 / math.sqrt(HEAD_DIM)
    key_heads = head_view(pieces[0][0])
    value_heads = head_view(pieces[1][0])
    allowed = pair_mask(own_group, group_all)
    scores = (
        jnp.einsum("qhe,khe->hqk", query_heads, key_heads, preferred_element_type=jnp.float32)
        * score_scale
    )
    masked = jnp.where(allowed, scores, NEG_LARGE)
    probs = jnp.where(allowed, jnp.exp(masked - log_norm[:, :, None]), 0.0)
    dprobs = jnp.einsum("qhe,khe->hqk", grad_heads, value_heads, preferred_element_type=jnp.float32)
    dscores = (probs * (dprobs - delta[:, :, None])).astype(jnp.bfloat16)
    return (
        jnp.einsum("hqk,khe->qhe", dscores, key_heads, preferred_element_type=jnp.float32)
        * score_scale
    )


def key_grad_block(own_keys, own_values, own_group, group_all, log_all, delta_all, pieces):
    score_scale = 1.0 / math.sqrt(HEAD_DIM)
    query_heads = head_view(pieces[0][0])
    grad_heads = head_view(pieces[1][0])
    allowed = pair_mask(group_all, own_group)
    scores = (
        jnp.einsum("qhe,khe->hqk", query_heads, own_keys, preferred_element_type=jnp.float32)
        * score_scale
    )
    masked = jnp.where(allowed, scores, NEG_LARGE)
    probs = jnp.where(allowed, jnp.exp(masked - log_all[:, :, None]), 0.0)
    grad_values = jnp.einsum(
        "hqk,qhe->khe", probs.astype(jnp.bfloat16), grad_heads, preferred_element_type=jnp.float32
    )
    dprobs = jnp.einsum("qhe,khe->hqk", grad_heads, own_values, preferred_element_type=jnp.float32)
    dscores = (probs * (dprobs - delta_all[:, :, None])).astype(jnp.bfloat16)
    grad_keys = (
        jnp.einsum("hqk,qhe->khe", dscores, query_heads, preferred_element_type=jnp.float32)
        * score_scale
    )
    return (grad_keys, grad_values)


def local(query_rows, key_rows, value_rows, out_weight, target, lengths, segments):
    own_rows = query_rows.shape[1]
    members = lax.axis_size(PATCH)
    groups = lax.axis_size(DP)
    total_rows = own_rows * members
    length = lengths[0]
    count = of_everyone(length.astype(jnp.float32), DP)
    offset = lax.axis_index(PATCH) * own_rows
    own_live = offset + lax.iota(jnp.int32, own_rows) < length
    segment_all = lax.all_gather(segments, PATCH, axis=1, tiled=True)
    group_all = jnp.where(lax.iota(jnp.int32, total_rows) < length, segment_all[0], -1)
    own_group = lax.dynamic_slice_in_dim(group_all, offset, own_rows, 0)
    query_heads = head_view(query_rows[0])
    starting = (
        jnp.full((HEADS, own_rows), NEG_LARGE, jnp.float32),
        jnp.zeros((HEADS, own_rows), jnp.float32),
        jnp.zeros((own_rows, HEADS, HEAD_DIM), jnp.float32),
    )
    forward_state = forward_block(
        starting,
        query_heads,
        own_group,
        group_all,
        sent_together((key_rows, value_rows), PATCH, 1, 0),
    )
    run_max, run_denom, run_accum = forward_state
    log_norm = run_max + jnp.log(run_denom)
    attn = (run_accum / run_denom.T[:, :, None]).reshape(own_rows, FEAT).astype(jnp.bfloat16)
    output = jnp.dot(attn, out_weight, preferred_element_type=jnp.float32)
    error = jnp.where(own_live[:, None], output - target[0].astype(jnp.float32), 0.0)
    loss_part = jnp.sum(error * error)
    grad_out = (2.0 * error).astype(jnp.bfloat16)
    weight_part = jnp.einsum("tf,td->fd", attn, grad_out, preferred_element_type=jnp.float32)
    grad_attn = jnp.einsum(
        "td,fd->tf", grad_out, out_weight, preferred_element_type=jnp.float32
    ).astype(jnp.bfloat16)
    delta = jnp.sum(
        (grad_attn.astype(jnp.float32) * attn.astype(jnp.float32)).reshape(
            own_rows, HEADS, HEAD_DIM
        ),
        axis=2,
    ).T
    grad_heads = head_view(grad_attn)
    query_raw = query_grad_block(
        query_heads,
        grad_heads,
        log_norm,
        delta,
        own_group,
        group_all,
        sent_together((key_rows, value_rows), PATCH, 1, 0),
    )
    log_all, delta_all = sent_together((log_norm, delta), PATCH, 1, 0)
    own_keys = head_view(key_rows[0])
    own_values = head_view(value_rows[0])
    key_raw, value_raw = key_grad_block(
        own_keys,
        own_values,
        own_group,
        group_all,
        log_all,
        delta_all,
        sent_together((query_rows, grad_attn[None]), PATCH, 1, 0),
    )
    loss_total = by_axis(loss_part, DP_PATCH)
    row_share = sum_at_owner(weight_part.astype(jnp.bfloat16), PATCH, 0)
    weight_share = sum_at_owner(row_share.astype(jnp.bfloat16), DP, 1)
    ratio = jnp.float32(groups * total_rows) / count
    query_grad = (ratio * query_raw).reshape(1, own_rows, FEAT)
    key_grad = (ratio * key_raw).reshape(1, own_rows, FEAT)
    value_grad = (ratio * value_raw).reshape(1, own_rows, FEAT)
    weight_grad = weight_share * (ratio / total_rows)
    loss = loss_total / (count * WIDTH)
    return (query_grad, key_grad, value_grad, weight_grad, loss)


def solution(mesh):
    torus = Mesh(mesh.devices.reshape(4, 8, 8, 2), ("dp_0", "dp_1", "patch_0", "patch_1"))
    return jax.shard_map(
        local,
        mesh=torus,
        in_specs=(
            P(DP, PATCH, None),
            P(DP, PATCH, None),
            P(DP, PATCH, None),
            P(),
            P(DP, PATCH, None),
            P(DP),
            P(DP, PATCH),
        ),
        out_specs=(P(DP, PATCH, None), P(DP, PATCH, None), P(DP, PATCH, None), P(PATCH, DP), P()),
        check_vma=False,
    )
```

profile of v0, /device:TPU:1, one launch (start us, length us, event | category | flops | bytes accessed | tf_op | source)
XLA Modules:
  0.0 233.7 jit_solution(14534418018708874223)
XLA Ops:
  7.2 1.8 pad_maximum_fusion
  9.8 21.1 %all_gather.14 = s32[1,2048]{1,0:T(1,128)S(1)} all-gather(s32[1,128]{1,0:T(1,128)} %param.13), channel_id=1, replica_groups=mesh['dp_0'=4,'dp_1'=8,'patch_0'=8,'patch_1'=2] {'patch_0','patch_1'}, dimensions={1}, use_global_device_ids=true | all-gather | bytes 8704 | tf_op jit(solution)/shard_map/all_gather | solution.py:138
  31.3 40.1 %all-gather.3.cloned.1.call-done = bf16[2,2048,576]{1,2,0:T(8,128)(2,1)} async-done(((bf16[2,128,576]{1,2,0:T(8,128)(2,1)}), bf16[2,2048,576]{1,2,0:T(8,128)(2,1)}) %all-gather.3.cloned.1.call-update) | async-done | bytes 4718608 | tf_op jit(solution)/shard_map/all_gather | solution.py:36
  71.4 2.8 %fusion.46 = (bf16[1,2048,576]{1,2,0:T(8,128)(2,1)S(1)}, bf16[1,2048,576]{1,2,0:T(8,128)(2,1)S(1)}) fusion(bf16[2,2048,576]{1,2,0:T(8,128)(2,1)} %all-gather.3.cloned.1.call-done), kind=kLoop, calls=%fused_computation.58 | loop fusion | bytes 9437184 | tf_op jit(solution)/shard_map/split | solution.py:36
  74.2 2.2 fusion.3
  76.3 2.0 fusion.1
  78.4 2.9 %fusion.27 = bf16[128,8,72]{0,2,1:T(8,128)(2,1)S(1)} fusion(bf16[2048,8,72]{0,2,1:T(8,128)(2,1)S(1)} %bitcast.87, f32[8,2048,128]{2,1,0:T(8,128)S(1)} %get-tuple-element.14, f32[8,128]{1,0:T(8,128)S(1)} %broadcast_maximum_fusion, pred[128,2048]{0,1:T(8,128)(4,1)S(1)} %broadcast_compare_fusion.1, f32[128,8]{0,1:T(8,128)S(1)} %bitcast.102, ...), kind=kOutput, calls=%fused_computation.25 | convolution fusion | flops 312696832 | bytes 11169792 | tf_op jit(solution)/shard_map/hqk,khe->qhe/dot_general | solution.py:80
  81.4 1.1 multiply_reduce_fusion
  82.5 1.2 convert_multiply_fusion
  83.7 0.8 pad_maximum_fusion.1
  85.1 8.3 %all-to-all-start = ((f32[32,1,1]{2,1,0:T(1,128)}), f32[32,1,1]{2,1,0:T(1,128)S(1)}, u32[]{:S(2)}, u32[]{:S(2)}) async-start(f32[32,1,1]{2,1,0:T(1,128)} %broadcast_in_dim.100), calls=%async_computation | async-start | bytes 32768 | tf_op jit(solution)/shard_map/all_to_all | solution.py:23
  93.4 1.4 convolution_convert_fusion
  94.8 1.3 reshape.133
  96.1 5.9 %all-to-all-done = f32[32,1,1]{2,1,0:T(1,128)S(1)} async-done(((f32[32,1,1]{2,1,0:T(1,128)}), f32[32,1,1]{2,1,0:T(1,128)S(1)}, u32[]{:S(2)}, u32[]{:S(2)}) %all-to-all-start) | async-done | bytes 160 | tf_op jit(solution)/shard_map/all_to_all | solution.py:23
  102.0 6.7 %all-to-all-start.1 = ((bf16[16,36,1152]{2,1,0:T(8,128)(2,1)}), bf16[16,36,1152]{2,1,0:T(8,128)(2,1)S(1)}, u32[]{:S(2)}, u32[]{:S(2)}) async-start(bf16[16,36,1152]{2,1,0:T(8,128)(2,1)} %reshape.133), calls=%async_computation.1 | async-start | bytes 2949120 | tf_op jit(solution)/shard_map/all_to_all | solution.py:53
  108.8 1.0 broadcast_compare_fusion
  109.8 0.6 reduce_sum.59
  111.1 8.2 %psum.28 = f32[]{:T(128)} all-reduce(f32[]{:T(128)} %get-tuple-element.17), channel_id=1, replica_groups=mesh['dp_0'=4,'dp_1'=8,'patch_0'=8,'patch_1'=2] {'dp_0'}, use_global_device_ids=true, to_apply=%region_7.8 | all-reduce | flops 1 | bytes 8 | tf_op jit(solution)/shard_map/psum | solution.py:41
  119.3 13.3 %psum.29 = f32[]{:T(128)} all-reduce(f32[]{:T(128)} %psum.28), channel_id=1, replica_groups=mesh['dp_0'=4,'dp_1'=8,'patch_0'=8,'patch_1'=2] {'dp_1'}, use_global_device_ids=true, to_apply=%region_8.9 | all-reduce | flops 1 | bytes 8 | tf_op jit(solution)/shard_map/psum | solution.py:41
  133.3 30.3 %psum.30 = f32[]{:T(128)} all-reduce(f32[]{:T(128)} %psum.29), channel_id=1, replica_groups=mesh['dp_0'=4,'dp_1'=8,'patch_0'=8,'patch_1'=2] {'patch_0'}, use_global_device_ids=true, to_apply=%region_9.10 | all-reduce | flops 1 | bytes 8 | tf_op jit(solution)/shard_map/psum | solution.py:41
  163.6 1.0 reduce_sum.58
  164.6 17.3 %all_gather.16 = f32[16,2048]{1,0:T(8,128)S(1)} all-gather(f32[16,128]{1,0:T(8,128)S(1)} %pad_maximum_fusion.2), channel_id=1, replica_groups=mesh['dp_0'=4,'dp_1'=8,'patch_0'=8,'patch_1'=2] {'patch_0','patch_1'}, dimensions={1}, use_global_device_ids=true | all-gather | bytes 139264 | tf_op jit(solution)/shard_map/all_gather | solution.py:36
  182.0 9.7 %fusion.20 = f32[8,72,128]{2,1,0:T(8,128)} fusion(bf16[2048,8,72]{0,2,1:T(8,128)(2,1)} %bitcast.84, f32[8,2048,128]{2,1,0:T(8,128)} %copy-done.1, bf16[128,8,72]{0,2,1:T(8,128)(2,1)} %bitcast.96, bf16[2048,8,72]{0,2,1:T(8,128)(2,1)} %bitcast.88, f32[8,128]{1,0:T(8,128)S(1)} %bitcast.104, f32[8,128]{1,0:T(8,128)S(1)} %get-tuple-element.11, ...), kind=kOutput, calls=%fused_computation.21 | convolution fusion | flops 618733568 | bytes 13819908 | tf_op jit(solution)/shard_map/hqk,khe->qhe/dot_general | solution.py:101
  192.0 0.8 reshape.134
  192.9 1.0 reshape.136
  193.9 3.9 %all-to-all-start.2 = ((bf16[32,2,648]{2,1,0:T(2,128)(2,1)}), bf16[32,2,648]{2,1,0:T(2,128)(2,1)S(1)}, u32[]{:S(2)}, u32[]{:S(2)}) async-start(bf16[32,2,648]{2,1,0:T(2,128)(2,1)} %reshape.136), calls=%async_computation.2 | async-start | bytes 196608 | tf_op jit(solution)/shard_map/all_to_all | solution.py:53
  197.8 3.3 %psum.31 = f32[]{:T(128)} all-reduce(f32[]{:T(128)} %psum.30), channel_id=1, replica_groups=mesh['dp_0'=4,'dp_1'=8,'patch_0'=8,'patch_1'=2] {'patch_1'}, use_global_device_ids=true, to_apply=%region_10.11 | all-reduce | flops 1 | bytes 8 | tf_op jit(solution)/shard_map/psum | solution.py:41
  201.8 5.0 %all-to-all-done.2 = bf16[32,2,648]{2,1,0:T(2,128)(2,1)S(1)} async-done(((bf16[32,2,648]{2,1,0:T(2,128)(2,1)}), bf16[32,2,648]{2,1,0:T(2,128)(2,1)S(1)}, u32[]{:S(2)}, u32[]{:S(2)}) %all-to-all-start.2) | async-done | bytes 82976 | tf_op jit(solution)/shard_map/all_to_all | solution.py:53
  207.9 2.8 %fusion.45 = (bf16[1,2048,576]{1,2,0:T(8,128)(2,1)S(1)}, bf16[1,2048,576]{1,2,0:T(8,128)(2,1)S(1)}) fusion(bf16[2,2048,576]{1,2,0:T(8,128)(2,1)} %all-gather.5.cloned.1.call-done), kind=kLoop, calls=%fused_computation.57 | loop fusion | bytes 9437184 | tf_op jit(solution)/shard_map/split | solution.py:36
  210.7 1.5 fusion.48
  212.2 3.9 %fusion.21 = f32[8,72,128]{2,1,0:T(8,128)} fusion(bf16[2048,8,72]{0,2,1:T(8,128)(2,1)S(1)} %bitcast.89, f32[8,2048,128]{2,1,0:T(8,128)S(1)} %fusion.48, f32[8,2048]{1,0:T(8,128)S(1)} %get-tuple-element.9, pred[2048,128]{1,0:T(8,128)(4,1)S(1)} %copy-done.12, f32[]{:T(128)S(6)} %div.19), kind=kOutput, calls=%fused_computation.22 | convolution fusion | flops 312549376 | bytes 11370500 | tf_op jit(solution)/shard_map/hqk,qhe->khe/dot_general | solution.py:117
  216.1 9.6 %fusion.19 = f32[8,72,128]{2,1,0:T(8,128)} fusion(bf16[2048,8,72]{0,2,1:T(8,128)(2,1)} %bitcast.86, f32[8,2048,128]{2,1,0:T(8,128)} %copy-done.4, bf16[2048,8,72]{0,2,1:T(8,128)(2,1)} %bitcast.90, bf16[128,8,72]{0,2,1:T(8,128)(2,1)S(1)} %bitcast.99, f32[8,2048]{1,0:T(8,128)S(1)} %get-tuple-element.10, f32[8,2048]{1,0:T(8,128)S(1)} %get-tuple-element.9, ...), kind=kOutput, calls=%fused_computation.20 | convolution fusion | flops 618733568 | bytes 13942788 | tf_op jit(solution)/shard_map/hqk,qhe->khe/dot_general | solution.py:123
  (49 shorter events, 2.7 us)
Async XLA Ops:
  7.2 74.2 %copy-start = (bf16[576,1152]{1,0:T(8,128)(2,1)S(1)}, bf16[576,1152]{1,0:T(8,128)(2,1)}, u32[]{:S(2)}) copy-start(bf16[576,1152]{1,0:T(8,128)(2,1)} %param.10) | copy-start | bytes 3981316
  7.2 67.0 %copy-start.9 = (bf16[1,128,576]{1,2,0:T(8,128)(2,1)S(1)}, bf16[1,128,576]{1,2,0:T(8,128)(2,1)}, u32[]{:S(2)}) copy-start(bf16[1,128,576]{1,2,0:T(8,128)(2,1)} %param.7) | copy-start | bytes 442372
  7.2 64.2 %all-gather.3.cloned.1.call-start = ((), (), s32[]{:S(2)}) async-start(), calls=%async_computation.3 | async-start | bytes 5013504 | tf_op jit(solution)/shard_map/all_gather | solution.py:36
  9.1 198.8 %all-gather.5.cloned.1.call-start = ((), (), s32[]{:S(2)}) async-start(), calls=%async_computation.4 | async-start | bytes 5013504 | tf_op jit(solution)/shard_map/all_gather | solution.py:36
  74.1 4.3 %copy-start.2 = (bf16[1,2048,576]{1,2,0:T(8,128)(2,1)}, bf16[1,2048,576]{1,2,0:T(8,128)(2,1)S(1)}, u32[]{:S(2)}) copy-start(bf16[1,2048,576]{1,2,0:T(8,128)(2,1)S(1)} %get-tuple-element.8) | copy-start | bytes 7077892
  74.1 4.3 %copy-start.5 = (bf16[1,2048,576]{1,2,0:T(8,128)(2,1)}, bf16[1,2048,576]{1,2,0:T(8,128)(2,1)S(1)}, u32[]{:S(2)}) copy-start(bf16[1,2048,576]{1,2,0:T(8,128)(2,1)S(1)} %get-tuple-element.7) | copy-start | bytes 7077892
  76.3 5.0 %copy-start.1 = (f32[8,2048,128]{2,1,0:T(8,128)}, f32[8,2048,128]{2,1,0:T(8,128)S(1)}, u32[]{:S(2)}) copy-start(f32[8,2048,128]{2,1,0:T(8,128)S(1)} %get-tuple-element.14) | copy-start | bytes 25165828
  78.4 3.0 %copy-start.11 = (bf16[1,128,1152]{2,1,0:T(8,128)(2,1)S(1)}, bf16[1,128,1152]{2,1,0:T(8,128)(2,1)}, u32[]{:S(2)}) copy-start(bf16[1,128,1152]{2,1,0:T(8,128)(2,1)} %param.11) | copy-start | bytes 884740
  81.4 3.8 %copy-start.7 = (bf16[128,8,72]{0,2,1:T(8,128)(2,1)}, bf16[128,8,72]{0,2,1:T(8,128)(2,1)S(1)}, u32[]{:S(2)}) copy-start(bf16[128,8,72]{0,2,1:T(8,128)(2,1)S(1)} %fusion.27) | copy-start | bytes 442372
  83.7 1.4 copy-start.8
  85.1 16.9 %all-to-all-start = ((f32[32,1,1]{2,1,0:T(1,128)}), f32[32,1,1]{2,1,0:T(1,128)S(1)}, u32[]{:S(2)}, u32[]{:S(2)}) async-start(f32[32,1,1]{2,1,0:T(1,128)} %broadcast_in_dim.100), calls=%async_computation | async-start | bytes 32768 | tf_op jit(solution)/shard_map/all_to_all | solution.py:23
  102.0 89.7 %all-to-all-start.1 = ((bf16[16,36,1152]{2,1,0:T(8,128)(2,1)}), bf16[16,36,1152]{2,1,0:T(8,128)(2,1)S(1)}, u32[]{:S(2)}, u32[]{:S(2)}) async-start(bf16[16,36,1152]{2,1,0:T(8,128)(2,1)} %reshape.133), calls=%async_computation.1 | async-start | bytes 2949120 | tf_op jit(solution)/shard_map/all_to_all | solution.py:53
  191.7 19.0 %copy-start.10 = (bf16[1,128,576]{1,2,0:T(8,128)(2,1)S(1)}, bf16[1,128,576]{1,2,0:T(8,128)(2,1)}, u32[]{:S(2)}) copy-start(bf16[1,128,576]{1,2,0:T(8,128)(2,1)} %param.8) | copy-start | bytes 442372
  193.9 12.9 %all-to-all-start.2 = ((bf16[32,2,648]{2,1,0:T(2,128)(2,1)}), bf16[32,2,648]{2,1,0:T(2,128)(2,1)S(1)}, u32[]{:S(2)}, u32[]{:S(2)}) async-start(bf16[32,2,648]{2,1,0:T(2,128)(2,1)} %reshape.136), calls=%async_computation.2 | async-start | bytes 196608 | tf_op jit(solution)/shard_map/all_to_all | solution.py:53
  207.9 4.3 %copy-start.12 = (pred[2048,128]{1,0:T(8,128)(4,1)S(1)}, pred[2048,128]{1,0:T(8,128)(4,1)}, u32[]{:S(2)}) copy-start(pred[2048,128]{1,0:T(8,128)(4,1)} %broadcast_compare_fusion) | copy-start | bytes 786436
  210.7 5.4 %copy-start.3 = (bf16[1,2048,576]{1,2,0:T(8,128)(2,1)}, bf16[1,2048,576]{1,2,0:T(8,128)(2,1)S(1)}, u32[]{:S(2)}) copy-start(bf16[1,2048,576]{1,2,0:T(8,128)(2,1)S(1)} %get-tuple-element.6) | copy-start | bytes 7077892
  210.7 5.4 %copy-start.6 = (bf16[1,2048,576]{1,2,0:T(8,128)(2,1)}, bf16[1,2048,576]{1,2,0:T(8,128)(2,1)S(1)}, u32[]{:S(2)}) copy-start(bf16[1,2048,576]{1,2,0:T(8,128)(2,1)S(1)} %get-tuple-element.5) | copy-start | bytes 7077892
  212.2 3.9 %copy-start.4 = (f32[8,2048,128]{2,1,0:T(8,128)}, f32[8,2048,128]{2,1,0:T(8,128)S(1)}, u32[]{:S(2)}) copy-start(f32[8,2048,128]{2,1,0:T(8,128)S(1)} %fusion.48) | copy-start | bytes 25165828
  212.2 3.9 %copy-start.13 = (bf16[1,128,576]{1,2,0:T(8,128)(2,1)S(1)}, bf16[1,128,576]{1,2,0:T(8,128)(2,1)}, u32[]{:S(2)}) copy-start(bf16[1,128,576]{1,2,0:T(8,128)(2,1)} %param.9) | copy-start | bytes 442372
Sparse Core Ops, SparseCore 0:
  10.6 60.7 all-gather.2
  84.6 78.2 all-gather.4
where the time goes:
time: 235 us; the launch traced here: 234 us
  blocking collectives  93.6 us (40%)
  waiting for transfers between devices  51 us (22%)
  matrix products  33.5 us (14%)
  starting transfers between devices  19 us (8%)
  between operations  18.1 us (8%)
  local copies, waits for them, and re-layouts  9.96 us (4%)
  other arithmetic  8.61 us (4%)
    psum x4, blocking collectives, by_axis(): value = lax.psum(value, axis)  55.2 us
    all_gather x2, waiting for transfers between devices, sent_together(): lax.all_gather(both, axis, axis=dim, tiled=True)  40.1 us
    all_gather x1, blocking collectives, local(): segment_all = lax.all_gather(segments, PATCH, axis=1, tiled=True)  21.1 us
    all_gather x1, blocking collectives, sent_together(): lax.all_gather(both, axis, axis=dim, tiled=True)  17.3 us
    all_to_all x2, starting transfers between devices, sum_at_owner(): lax.all_to_all(in_blocks(value, dim, peers), axis, 0, 0, tiled=True)  10.6 us
    dot_general x1, matrix products, query_grad_block(): jnp.einsum('hqk,khe->qhe', dscores, key_heads, preferred_element_type=jnp...  9.73 us
    dot_general x1, matrix products, key_grad_block(): jnp.einsum('hqk,qhe->khe', dscores, query_heads, preferred_element_type=j...  9.62 us
    all_to_all x1, starting transfers between devices, from_everyone(): return lax.all_to_all(copies, axis, split_axis=0, concat_axis=0, tiled=True)  8.3 us
  transfers between devices with their start and end apart: 5, of which 3 were waited for; matrix products, arithmetic and copies ran while one was open for 8% of the time, Pallas kernels for 0%

commit v1 on v0

v1 whole, which is shorter than its diff:
```python
import functools
import math

import jax
import jax.numpy as jnp
from jax import lax
from jax.experimental import pallas as pl
from jax.experimental.pallas import tpu as pltpu
from jax.sharding import Mesh
from jax.sharding import PartitionSpec as P

WIDTH = 1152
HEADS = 8
HEAD_DIM = 72
FEAT = 576
TOK = 128
HP = 80
FP = HEADS * HP
PATCH = ("patch_0", "patch_1")
DP = ("dp_0", "dp_1")
DP_PATCH = ("dp_0", "dp_1", "patch_0", "patch_1")
NEG_LARGE = -1e30
MESH = pl.DeviceIdType.MESH
BF = jnp.bfloat16
F32 = jnp.float32
ORDER = (4, 3, 5, 2, 6, 1, 7)
QTILE = 256
TILES = 4
KCH = 256
CHUNKS = 8


def mm(a, b):
    return jnp.dot(a, b, preferred_element_type=F32)


def mmt(a, b):
    return lax.dot_general(a, b, (((1,), (1,)), ((), ())), preferred_element_type=F32)


def eye(n):
    r = lax.broadcasted_iota(jnp.int32, (n, n), 0)
    c = lax.broadcasted_iota(jnp.int32, (n, n), 1)
    return jnp.where(r == c, 1.0, 0.0).astype(BF)


def lanes(i, n):
    return pl.ds(pl.multiple_of(i * n, n), n)


def kernel(
    q_ref, k_ref, v_ref, w_ref, tgt_ref, len_ref, seg_ref,
    dq_ref, dk_ref, dv_ref, attn_out, gt_out, loss_ref,
    e_ref, snd, rx, sib, segs, qt, kt, vt, km, vm, gk, gq, s_ref, p_ref, ds_ref, rden,
    w_pad, w_tr, tgt_tr, attn_snd, attn_rx, go_snd, go_rx, gos, q_snd, xs_snd, xs_rx, own,
    kv_snd, grad_rx,
    ssem, rsem,
):
    y = lax.axis_index("patch_0")
    c = lax.axis_index("patch_1")
    chip = lambda d: lax.rem(y + d, 8)
    at = lambda h: {"patch_0": h}
    sibling = {"patch_1": 1 - c}
    barrier = pltpu.get_barrier_semaphore()
    for d in range(1, 8):
        pl.semaphore_signal(barrier, inc=1, device_id=at(chip(d)), device_id_type=MESH)
    pl.semaphore_signal(barrier, inc=1, device_id=sibling, device_id_type=MESH)

    def send(kind, slot, src, dst, to, dslot):
        return pltpu.make_async_remote_copy(
            src_ref=src, dst_ref=dst, send_sem=ssem.at[kind, slot], recv_sem=rsem.at[kind, dslot],
            device_id=to, device_id_type=MESH)

    for h in range(HEADS):
        r = lax.broadcasted_iota(jnp.int32, (HP, FEAT), 0)
        f = lax.broadcasted_iota(jnp.int32, (HP, FEAT), 1)
        hit = jnp.logical_and(f - r == HEAD_DIM * h, r < HEAD_DIM)
        e_ref[h * HP:(h + 1) * HP, :] = jnp.where(hit, 1.0, 0.0).astype(BF)
    spread = e_ref[...]
    for j, ref in enumerate((q_ref, k_ref, v_ref)):
        snd[:, j * HP:(j + 1) * HP, :] = mmt(spread, ref[...]).astype(BF).reshape(HEADS, HP, TOK)
    segs[0, y] = seg_ref[...]
    rx[y] = snd[y]

    pl.semaphore_wait(barrier, 8)
    for d in ORDER:
        h = chip(d)
        send(0, h, snd.at[h], rx.at[y], at(h), y).start()
        send(1, h, seg_ref, segs.at[0, y], at(h), y).start()
    send(2, y, snd.at[y, HP:3 * HP], sib.at[y], sibling, y).start()
    send(3, y, seg_ref, segs.at[1, y], sibling, y).start()

    id256 = eye(256)
    id128 = eye(128)
    w_pad[...] = mm(spread, w_ref[...]).astype(BF)
    for j in range(5):
        n = 256 if j < 4 else 128
        cols = slice(256 * j, 256 * j + n)
        unit = id256 if n == 256 else id128
        w_tr[cols, :] = mmt(unit, w_pad[:, cols]).astype(BF)
        tgt_tr[cols, :] = mmt(unit, tgt_ref[:, cols]).astype(BF)
    length = len_ref[0]

    def place(block, number, parity, source, kv_t):
        kb, vb = kv_t[0:HP], kv_t[HP:2 * HP]
        kt[:, lanes(block, TOK)] = kb
        vt[:, lanes(block, TOK)] = vb
        rows = lanes(block, TOK)
        km[rows, :] = mmt(id128, kb).astype(BF)
        vm[rows, :] = mmt(id128, vb).astype(BF)
        at_pos = number * TOK + lax.broadcasted_iota(jnp.int32, (1, TOK), 1)
        group = jnp.where(at_pos < length, segs[parity, source], -1).astype(F32)
        spread_rows = jnp.broadcast_to(group, (TOK, TOK)).astype(BF)
        gk[rows, :] = mmt(id128, spread_rows)
        return group

    def place_own(source):
        block = rx[source]
        qt[:, lanes(source, TOK)] = block[0:HP]
        group = place(source, 2 * source + c, 0, source, block[HP:3 * HP])
        gq[:, lanes(source, TOK)] = group

    place_own(y)
    for d in ORDER:
        s = chip(d)
        send(0, s, snd.at[s], rx.at[s], at(s), s).wait_recv()
        send(1, s, seg_ref, segs.at[0, s], at(s), s).wait_recv()
        send(2, s, rx.at[s, HP:3 * HP], sib.at[s], sibling, s).start()
        send(3, s, segs.at[0, s], segs.at[1, s], sibling, s).start()
        place_own(s)
    for d in (0,) + ORDER:
        s = chip(d)
        send(2, s, rx.at[s, HP:3 * HP], sib.at[s], sibling, s).wait_recv()
        send(3, s, segs.at[0, s], segs.at[1, s], sibling, s).wait_recv()
        place(8 + s, 2 * s + 1 - c, 1, s, sib[s])

    scale = 1.0 / math.sqrt(HEAD_DIM)
    to_two = scale / math.log(2.0)

    def chunk(i):
        return pl.ds(pl.multiple_of(i * KCH, KCH), KCH)

    @pl.loop(0, TILES)
    def _(t):
        own_q = qt[:, lanes(t, QTILE)]
        own_g = gq[:, lanes(t, QTILE)]

        def first(i, top):
            sc = mm(km[chunk(i), :], own_q)
            g = gk[chunk(i), :]
            sc = jnp.where(jnp.concatenate([g, g], axis=1) == own_g, sc, NEG_LARGE)
            s_ref[chunk(i), :] = sc
            return jnp.maximum(top, jnp.max(sc, axis=0, keepdims=True))

        top = lax.fori_loop(0, CHUNKS, first, jnp.full((1, QTILE), NEG_LARGE, F32))

        def second(i, total):
            pr = jnp.exp2((s_ref[chunk(i), :] - top) * to_two)
            p_ref[t, chunk(i), :] = pr.astype(BF)
            return total + jnp.sum(pr, axis=0, keepdims=True)

        total = lax.fori_loop(0, CHUNKS, second, jnp.zeros((1, QTILE), F32))
        inv = 1.0 / total
        rden[t] = inv
        out = (mm(vt[...], p_ref[t]) * inv).astype(BF)
        for half in range(2):
            b = 2 * t + half
            attn_snd[b] = out[:, half * TOK:(half + 1) * TOK]

            @pl.when(b != y)
            def _():
                send(4, b, attn_snd.at[b], attn_rx.at[y], at(b), y).start()

    attn_rx[y] = attn_snd[y]
    for d in ORDER:
        s = chip(d)
        send(4, s, attn_snd.at[s], attn_rx.at[s], at(s), s).wait_recv()

    attn_t = attn_rx[...].reshape(FP, TOK)
    position = (2 * y + c) * TOK + lax.broadcasted_iota(jnp.int32, (1, TOK), 1)
    live = position < length
    out_t = mm(w_tr[...], attn_t)
    error = jnp.where(live, out_t - tgt_tr[...].astype(F32), 0.0)
    grad_t = (2.0 * error).astype(BF)
    gt_out[...] = grad_t
    go_snd[...] = mm(w_pad[...], grad_t).astype(BF).reshape(HEADS, HP, TOK)
    for d in ORDER:
        h = chip(d)
        send(5, h, go_snd.at[h], go_rx.at[y], at(h), y).start()
    go_rx[y] = go_snd[y]
    attn_out[...] = attn_t
    loss_ref[...] = jnp.sum(error * error, axis=0, keepdims=True)

    @pl.loop(0, TILES)
    def _(t):
        for half in range(2):
            b = 2 * t + half

            @pl.when(b != y)
            def _():
                send(5, b, go_snd.at[b], go_rx.at[b], at(b), b).wait_recv()

        both = jnp.concatenate([go_rx[2 * t], go_rx[2 * t + 1]], axis=1).astype(F32)
        scaled = (both * rden[t]).astype(BF)
        gos[t] = scaled
        attn = jnp.concatenate([attn_snd[2 * t], attn_snd[2 * t + 1]], axis=1)
        delta = jnp.sum(scaled.astype(F32) * attn.astype(F32), axis=0, keepdims=True)

        @pl.loop(0, CHUNKS)
        def _(i):
            dp = mm(vm[chunk(i), :], scaled)
            ds_ref[t, chunk(i), :] = (p_ref[t, chunk(i), :].astype(F32) * (dp - delta)).astype(BF)

        dq = (mm(kt[...], ds_ref[t]) * scale).astype(BF)
        for half in range(2):
            b = 2 * t + half
            q_snd[b] = dq[:, half * TOK:(half + 1) * TOK]

            @pl.when(b != y)
            def _():
                send(6, b, q_snd.at[b], grad_rx.at[y, 0:HP], at(b), y).start()

    def key_value(i):
        dk = jnp.zeros((HP, KCH), F32)
        dv = jnp.zeros((HP, KCH), F32)
        for t in range(TILES):
            dk = dk + mmt(qt[:, t * QTILE:(t + 1) * QTILE], ds_ref[t, chunk(i), :])
            dv = dv + mmt(gos[t], p_ref[t, chunk(i), :])
        return dk * scale, dv

    @pl.loop(0, 4)
    def _(i):
        dk, dv = key_value(i + 4)
        for half in range(2):
            b = 2 * i + half
            cols = slice(half * TOK, (half + 1) * TOK)
            xs_snd[b, 0:HP] = dk[:, cols].astype(BF)
            xs_snd[b, HP:2 * HP] = dv[:, cols].astype(BF)
            send(7, b, xs_snd.at[b], xs_rx.at[b], sibling, b).start()

    @pl.loop(0, 4)
    def _(i):
        dk, dv = key_value(i)
        for half in range(2):
            b = 2 * i + half
            cols = slice(half * TOK, (half + 1) * TOK)
            send(7, b, xs_snd.at[b], xs_rx.at[b], sibling, b).wait_recv()
            kv_snd[b, 0:HP] = (dk[:, cols] + xs_rx[b, 0:HP].astype(F32)).astype(BF)
            kv_snd[b, HP:2 * HP] = (dv[:, cols] + xs_rx[b, HP:2 * HP].astype(F32)).astype(BF)

            @pl.when(b != y)
            def _():
                send(8, b, kv_snd.at[b], grad_rx.at[y, HP:3 * HP], at(b), y).start()

    grad_rx[y, 0:HP] = q_snd[y]
    grad_rx[y, HP:3 * HP] = kv_snd[y]
    compact = jnp.zeros((FEAT, FP), BF)
    rows = []
    for h in range(HEADS):
        f = lax.broadcasted_iota(jnp.int32, (HEAD_DIM, FP), 0)
        r = lax.broadcasted_iota(jnp.int32, (HEAD_DIM, FP), 1)
        rows.append(jnp.where(r - f == HP * h, 1.0, 0.0))
    compact = jnp.concatenate(rows, axis=0).astype(BF)
    for d in ORDER:
        s = chip(d)
        send(6, s, q_snd.at[s], grad_rx.at[s, 0:HP], at(s), s).wait_recv()
        send(8, s, kv_snd.at[s], grad_rx.at[s, HP:3 * HP], at(s), s).wait_recv()
    for j, ref in enumerate((dq_ref, dk_ref, dv_ref)):
        got = grad_rx[:, j * HP:(j + 1) * HP, :].reshape(FP, TOK)
        ref[...] = mmt(id128, mm(compact, got).astype(BF))

    for d in (0,) + ORDER:
        s = chip(d)
        if d:
            send(0, s, snd.at[s], rx.at[y], at(s), y).wait_send()
            send(1, s, seg_ref, segs.at[0, y], at(s), y).wait_send()
            send(4, s, attn_snd.at[s], attn_rx.at[y], at(s), y).wait_send()
            send(5, s, go_snd.at[s], go_rx.at[y], at(s), y).wait_send()
            send(6, s, q_snd.at[s], grad_rx.at[y, 0:HP], at(s), y).wait_send()
            send(8, s, kv_snd.at[s], grad_rx.at[y, HP:3 * HP], at(s), y).wait_send()
        send(2, s, rx.at[s, HP:3 * HP], sib.at[s], sibling, s).wait_send()
        send(3, s, segs.at[0, s], segs.at[1, s], sibling, s).wait_send()
        send(7, s, xs_snd.at[s], xs_rx.at[s], sibling, s).wait_send()


def attention(q, k, v, w, target, lengths, segments):
    vm = pltpu.VMEM
    vmem = pl.BlockSpec(memory_space=pltpu.VMEM)
    keys = 16 * TOK
    return pl.pallas_call(
        kernel,
        out_shape=[
            jax.ShapeDtypeStruct((TOK, FEAT), F32),
            jax.ShapeDtypeStruct((TOK, FEAT), F32),
            jax.ShapeDtypeStruct((TOK, FEAT), F32),
            jax.ShapeDtypeStruct((FP, TOK), BF),
            jax.ShapeDtypeStruct((WIDTH, TOK), BF),
            jax.ShapeDtypeStruct((1, TOK), F32),
        ],
        in_specs=[vmem] * 5 + [pl.BlockSpec(memory_space=pltpu.SMEM), vmem],
        out_specs=[vmem] * 6,
        scratch_shapes=[
            vm((FP, FEAT), BF),
            vm((HEADS, 3 * HP, TOK), BF),
            vm((HEADS, 3 * HP, TOK), BF),
            vm((HEADS, 2 * HP, TOK), BF),
            vm((2, HEADS, 1, TOK), jnp.int32),
            vm((HP, 8 * TOK), BF),
            vm((HP, keys), BF),
            vm((HP, keys), BF),
            vm((keys, HP), BF),
            vm((keys, HP), BF),
            vm((keys, TOK), F32),
            vm((1, 8 * TOK), F32),
            vm((keys, QTILE), F32),
            vm((TILES, keys, QTILE), BF),
            vm((TILES, keys, QTILE), BF),
            vm((TILES, 1, QTILE), F32),
            vm((FP, WIDTH), BF),
            vm((WIDTH, FP), BF),
            vm((WIDTH, TOK), BF),
            vm((HEADS, HP, TOK), BF),
            vm((HEADS, HP, TOK), BF),
            vm((HEADS, HP, TOK), BF),
            vm((HEADS, HP, TOK), BF),
            vm((TILES, HP, QTILE), BF),
            vm((HEADS, HP, TOK), BF),
            vm((HEADS, 2 * HP, TOK), BF),
            vm((HEADS, 2 * HP, TOK), BF),
            vm((HEADS, 2 * HP, TOK), F32),
            vm((HEADS, 2 * HP, TOK), BF),
            vm((HEADS, 3 * HP, TOK), BF),
            pltpu.SemaphoreType.DMA((9, HEADS)),
            pltpu.SemaphoreType.DMA((9, HEADS)),
        ],
        compiler_params=pltpu.CompilerParams(
            collective_id=0, has_side_effects=True, vmem_limit_bytes=48 * 1024 * 1024),
        name="attention",
    )(q, k, v, w, target, lengths, segments)


def from_everyone(value, axis):
    copies = jnp.broadcast_to(value, (lax.axis_size(axis), *value.shape))
    return lax.all_to_all(copies, axis, split_axis=0, concat_axis=0, tiled=True)


def of_everyone(value, axis):
    return from_everyone(value, axis).sum(axis=0)


def in_blocks(value, dim, peers):
    shape = value.shape
    pieces = value.reshape(*shape[:dim], peers, shape[dim] // peers, *shape[dim + 1:])
    return jnp.moveaxis(pieces, dim, 0)


def sum_at_owner(value, axis, dim):
    peers = lax.axis_size(axis)
    pieces = lax.all_to_all(in_blocks(value, dim, peers), axis, 0, 0, tiled=True)
    return jnp.sum(pieces.astype(F32), axis=0)


def local(query_rows, key_rows, value_rows, out_weight, target, lengths, segments):
    groups = lax.axis_size(DP)
    total_rows = TOK * lax.axis_size(PATCH)
    dq, dk, dv, attn_t, grad_t, loss_part = attention(
        query_rows[0], key_rows[0], value_rows[0], out_weight, target[0], lengths, segments)
    weight_part = lax.dot_general(
        attn_t.reshape(HEADS, HP, TOK)[:, :HEAD_DIM].reshape(FEAT, TOK), grad_t,
        (((1,), (1,)), ((), ())), preferred_element_type=F32)
    stats = jnp.stack([jnp.sum(loss_part), lengths[0].astype(F32)])
    stats = of_everyone(of_everyone(stats, PATCH), DP)
    count = stats[1] / lax.axis_size(PATCH)
    row_share = sum_at_owner(weight_part.astype(BF), PATCH, 0)
    weight_share = sum_at_owner(row_share.astype(BF), DP, 1)
    ratio = jnp.float32(groups * total_rows) / count
    return (
        (ratio * dq)[None], (ratio * dk)[None], (ratio * dv)[None],
        weight_share * (ratio / total_rows), stats[0] / (count * WIDTH))


def solution(mesh):
    torus = Mesh(mesh.devices.reshape(4, 8, 8, 2), ("dp_0", "dp_1", "patch_0", "patch_1"))
    return jax.shard_map(
        local,
        mesh=torus,
        in_specs=(P(DP, PATCH, None), P(DP, PATCH, None), P(DP, PATCH, None), P(),
                  P(DP, PATCH, None), P(DP), P(DP, PATCH)),
        out_specs=(P(DP, PATCH, None), P(DP, PATCH, None), P(DP, PATCH, None), P(PATCH, DP), P()),
        check_vma=False,
    )
```

time: 235 us -> 164 us (0.70)
  blocking collectives: 93.6 us -> 0 us
  Pallas kernels: 0 us -> 55.3 us
  matrix products: 33.5 us -> 0.5 us
  between operations: 18.1 us -> 4.5 us
  starting transfers between devices: 19 us -> 31.6 us
  other arithmetic: 8.61 us -> 2.42 us
  local copies, waits for them, and re-layouts: 9.96 us -> 14.2 us
  waiting for transfers between devices: 51 us -> 54.6 us
    pallas_call x0 -> x1, Pallas kernels: none -> 55.3 us  [attention(): pl.pallas_call(kernel, out_shape=[jax.ShapeDtypeStruct((TOK, FEAT), F32),...]
    psum x4 -> x0, blocking collectives: 55.2 us -> none  [by_axis(): value = lax.psum(value, axis)]
    all_gather x2 -> x0, waiting for transfers between devices: 40.1 us -> none  [sent_together(): lax.all_gather(both, axis, axis=dim, tiled=True)]
    all_gather x2 -> x0, blocking collectives: 38.4 us -> none  [the longest x1 21.1 us: local(): segment_all = lax.all_gather(segments, PATCH, axis=1, tiled=True)]
    all_to_all x2, waiting for transfers between devices: 5.01 us -> 40.8 us  [sum_at_owner(): lax.all_to_all(in_blocks(value, dim, peers), axis, 0, 0, tiled=True)]
    dot_general x9 -> x1, matrix products: 33.5 us -> 0.5 us  [local(): lax.dot_general(attn_t.reshape(HEADS, HP, TOK)[:, :HEAD_DIM].reshape(FEAT...]
    all_to_all x1 -> x2, starting transfers between devices: 8.3 us -> 22.2 us  [from_everyone(): return lax.all_to_all(copies, axis, split_axis=0, concat_axis=0, tiled=True)]
    unnamed x30 -> x14, local copies, waits for them, and re-layouts: 1.52 us -> 10.1 us
  transfers between devices with their start and end apart: 5 -> 4, of which waited for: 3 -> 4; matrix products, arithmetic and copies ran while one was open for 8% -> 3% of each run, Pallas kernels for 0% -> 0%
where the time goes in v1:
time: 164 us; the launch traced here: 163 us
  Pallas kernels  55.3 us (34%)
  waiting for transfers between devices  54.6 us (33%)
  starting transfers between devices  31.6 us (19%)
  local copies, waits for them, and re-layouts  14.2 us (9%)
  between operations  4.5 us (3%)
  other arithmetic  2.42 us (1%)
    pallas_call x1, Pallas kernels, attention(): pl.pallas_call(kernel, out_shape=[jax.ShapeDtypeStruct((TOK, FEAT), F32),...  55.3 us
    all_to_all x2, waiting for transfers between devices, sum_at_owner(): lax.all_to_all(in_blocks(value, dim, peers), axis, 0, 0, tiled=True)  40.8 us
    all_to_all x2, starting transfers between devices, from_everyone(): return lax.all_to_all(copies, axis, split_axis=0, concat_axis=0, tiled=True)  22.2 us
    all_to_all x2, waiting for transfers between devices, from_everyone(): return lax.all_to_all(copies, axis, split_axis=0, concat_axis=0, tiled=True)  13.8 us
    unnamed x14, local copies, waits for them, and re-layouts  10.1 us
    all_to_all x2, starting transfers between devices, sum_at_owner(): lax.all_to_all(in_blocks(value, dim, peers), axis, 0, 0, tiled=True)  9.44 us
  transfers between devices with their start and end apart: 4, of which 4 were waited for; matrix products, arithmetic and copies ran while one was open for 3% of the time, Pallas kernels for 0%

profile of v1, /device:TPU:1, one launch (start us, length us, event | category | flops | bytes accessed | tf_op | source)
XLA Modules:
  0.0 163.1 jit_solution(8435028924118113715)
XLA Ops:
  1.3 1.1 copy.44
  2.3 1.1 copy.45
  3.4 1.1 copy.46
  4.5 1.3 copy-done
  5.8 1.0 copy-done.1
  6.8 0.7 copy-done.2
  7.4 55.3 %attention.1 = (f32[128,576]{1,0:T(8,128)S(1)}, f32[128,576]{1,0:T(8,128)S(1)}, f32[128,576]{1,0:T(8,128)S(1)}, bf16[640,128]{1,0:T(8,128)(2,1)S(1)}, bf16[1152,...) custom-call(bf16[128,576]{1,0:T(8,128)(2,1)S(1)} %bitcast.18, bf16[128,576]{1,0:T(8,128)(2,1)S(1)} %bitcast.19, ...), custom_call_target="tpu_custom_call" | custom-call | tf_op jit(solution)/shard_map/attention/pallas_call | solution.py:290
  62.8 0.6 reduce_sum.48
  63.4 0.7 pad_maximum_fusion
  64.1 0.6 broadcast_in_dim.15
  64.7 9.0 %all-to-all-start = ((f32[16,1,2]{2,1,0:T(1,128)}), f32[16,1,2]{2,1,0:T(1,128)S(1)}, u32[]{:S(2)}, u32[]{:S(2)}) async-start(f32[16,1,2]{2,1,0:T(1,128)} %broadcast_in_dim.15), calls=%async_computation | async-start | bytes 16384 | tf_op jit(solution)/shard_map/all_to_all | solution.py:344
  73.7 7.0 %all-to-all-done = f32[16,1,2]{2,1,0:T(1,128)S(1)} async-done(((f32[16,1,2]{2,1,0:T(1,128)}), f32[16,1,2]{2,1,0:T(1,128)S(1)}, u32[]{:S(2)}, u32[]{:S(2)}) %all-to-all-start) | async-done | bytes 160 | tf_op jit(solution)/shard_map/all_to_all | solution.py:344
  80.7 0.6 broadcast_in_dim.16
  81.3 13.2 %all-to-all-start.1 = ((f32[32,1,2]{2,1,0:T(1,128)}), f32[32,1,2]{2,1,0:T(1,128)S(1)}, u32[]{:S(2)}, u32[]{:S(2)}) async-start(f32[32,1,2]{2,1,0:T(1,128)} %broadcast_in_dim.16), calls=%async_computation.1 | async-start | bytes 32768 | tf_op jit(solution)/shard_map/all_to_all | solution.py:344
  94.5 0.5 convolution_convert_fusion
  95.0 1.3 reshape.41
  96.3 6.8 %all-to-all-done.1 = f32[32,1,2]{2,1,0:T(1,128)S(1)} async-done(((f32[32,1,2]{2,1,0:T(1,128)}), f32[32,1,2]{2,1,0:T(1,128)S(1)}, u32[]{:S(2)}, u32[]{:S(2)}) %all-to-all-start.1) | async-done | bytes 288 | tf_op jit(solution)/shard_map/all_to_all | solution.py:344
  103.1 5.6 %all-to-all-start.2 = ((bf16[16,36,1152]{2,1,0:T(8,128)(2,1)}), bf16[16,36,1152]{2,1,0:T(8,128)(2,1)S(1)}, u32[]{:S(2)}, u32[]{:S(2)}) async-start(bf16[16,36,1152]{2,1,0:T(8,128)(2,1)} %reshape.41), calls=%async_computation.2 | async-start | bytes 2949120 | tf_op jit(solution)/shard_map/all_to_all | solution.py:359
  108.7 0.6 fusion
  110.7 0.9 copy.50
  111.6 33.7 %all-to-all-done.2 = bf16[16,36,1152]{2,1,0:T(8,128)(2,1)S(1)} async-done(((bf16[16,36,1152]{2,1,0:T(8,128)(2,1)}), bf16[16,36,1152]{2,1,0:T(8,128)(2,1)S(1)}, u32[]{:S(2)}, u32[]{:S(2)}) %all-to-all-start.2) | async-done | bytes 1327136 | tf_op jit(solution)/shard_map/all_to_all | solution.py:359
  145.3 0.2 reduce_sum.51
  145.5 0.8 reshape.42
  146.3 0.1 copy.49
  146.5 1.0 reshape.43
  147.5 3.9 %all-to-all-start.3 = ((bf16[32,2,648]{2,1,0:T(2,128)(2,1)}), bf16[32,2,648]{2,1,0:T(2,128)(2,1)S(1)}, u32[]{:S(2)}, u32[]{:S(2)}) async-start(bf16[32,2,648]{2,1,0:T(2,128)(2,1)} %reshape.43), calls=%async_computation.3 | async-start | bytes 196608 | tf_op jit(solution)/shard_map/all_to_all | solution.py:359
  151.4 0.9 copy.52
  152.2 0.9 copy.51
  153.8 7.1 %all-to-all-done.3 = bf16[32,2,648]{2,1,0:T(2,128)(2,1)S(1)} async-done(((bf16[32,2,648]{2,1,0:T(2,128)(2,1)}), bf16[32,2,648]{2,1,0:T(2,128)(2,1)S(1)}, u32[]{:S(2)}, u32[]{:S(2)}) %all-to-all-start.3) | async-done | bytes 82976 | tf_op jit(solution)/shard_map/all_to_all | solution.py:359
  160.9 0.4 reshape.44
  161.3 0.1 convert_reduce_fusion
  161.4 0.6 broadcast_multiply_fusion
  (8 shorter events, 0.2 us)
Async XLA Ops:
  4.5 1.3 copy-start
  5.8 1.0 copy-start.1
  6.8 0.7 copy-start.2
  64.7 16.0 %all-to-all-start = ((f32[16,1,2]{2,1,0:T(1,128)}), f32[16,1,2]{2,1,0:T(1,128)S(1)}, u32[]{:S(2)}, u32[]{:S(2)}) async-start(f32[16,1,2]{2,1,0:T(1,128)} %broadcast_in_dim.15), calls=%async_computation | async-start | bytes 16384 | tf_op jit(solution)/shard_map/all_to_all | solution.py:344
  81.3 21.8 %all-to-all-start.1 = ((f32[32,1,2]{2,1,0:T(1,128)}), f32[32,1,2]{2,1,0:T(1,128)S(1)}, u32[]{:S(2)}, u32[]{:S(2)}) async-start(f32[32,1,2]{2,1,0:T(1,128)} %broadcast_in_dim.16), calls=%async_computation.1 | async-start | bytes 32768 | tf_op jit(solution)/shard_map/all_to_all | solution.py:344
  103.1 42.2 %all-to-all-start.2 = ((bf16[16,36,1152]{2,1,0:T(8,128)(2,1)}), bf16[16,36,1152]{2,1,0:T(8,128)(2,1)S(1)}, u32[]{:S(2)}, u32[]{:S(2)}) async-start(bf16[16,36,1152]{2,1,0:T(8,128)(2,1)} %reshape.41), calls=%async_computation.2 | async-start | bytes 2949120 | tf_op jit(solution)/shard_map/all_to_all | solution.py:359
  147.5 13.4 %all-to-all-start.3 = ((bf16[32,2,648]{2,1,0:T(2,128)(2,1)}), bf16[32,2,648]{2,1,0:T(2,128)(2,1)S(1)}, u32[]{:S(2)}, u32[]{:S(2)}) async-start(bf16[32,2,648]{2,1,0:T(2,128)(2,1)} %reshape.43), calls=%async_computation.3 | async-start | bytes 196608 | tf_op jit(solution)/shard_map/all_to_all | solution.py:359

commit v2 on v1

v2 whole, which is shorter than its diff:
```python
import math

import jax
import jax.numpy as jnp
from jax import lax
from jax.experimental import pallas as pl
from jax.experimental.pallas import tpu as pltpu
from jax.sharding import Mesh
from jax.sharding import PartitionSpec as P

WIDTH = 1152
HEADS = 8
HEAD_DIM = 72
FEAT = 576
TOK = 128
HALF = 36
HALF_PAD = 48
LANES = HEADS * HALF_PAD
PATCH = ("patch_0", "patch_1")
DP = ("dp_0", "dp_1")
DP_PATCH = ("dp_0", "dp_1", "patch_0", "patch_1")
NEG_LARGE = -1e30
MESH = pl.DeviceIdType.MESH
BF = jnp.bfloat16
F32 = jnp.float32
ORDER = (4, 3, 5, 2, 6, 1, 7)
QTILE = 256
TILES = 4
KCH = 256
CHUNKS = 8


def mm(a, b):
    return jnp.dot(a, b, preferred_element_type=F32)


def mmt(a, b):
    return lax.dot_general(a, b, (((1,), (1,)), ((), ())), preferred_element_type=F32)


def eye(n):
    r = lax.broadcasted_iota(jnp.int32, (n, n), 0)
    c = lax.broadcasted_iota(jnp.int32, (n, n), 1)
    return jnp.where(r == c, 1.0, 0.0).astype(BF)


def lanes(i, n):
    return pl.ds(pl.multiple_of(i * n, n), n)


def up(n, m):
    return (n + m - 1) // m * m


def kernel(
    q_hbm, k_hbm, v_hbm, w_hbm, tgt_hbm, len_ref, seg_hbm,
    dq_ref, dk_ref, dv_ref, wg_ref, stat_ref,
    snd, w_ref, tgt_ref, rx, sib, segs, qt, kt, vt, km, vm, gk, gq, s_ref, p_ref, ds_ref, rden,
    w_tr, tgt_tr, attn_snd, attn_rx, go_snd, go_rx, gos, q_snd, xs_snd, xs_rx, kv_snd, grad_rx,
    gt, gt_sib, attn_sib, stats, x_snd, x_rx, x_sum, z_snd, z_rx, y_snd, y_rx,
    lsem, ssem, rsem,
):
    x = lax.axis_index("dp_0")
    z = lax.axis_index("dp_1")
    y = lax.axis_index("patch_0")
    c = lax.axis_index("patch_1")
    nx = lax.axis_size("dp_0")
    nz = lax.axis_size("dp_1")
    HD = HEAD_DIM
    chip = lambda d: lax.rem(y + d, 8)
    at = lambda h: {"patch_0": h}
    xs = [(lax.rem(x + d, nx)) for d in range(1, nx)]
    zs = [(lax.rem(z + d, nz)) for d in range(1, nz)]
    sibling = {"patch_1": 1 - c}
    barrier = pltpu.get_barrier_semaphore()
    for d in range(1, 8):
        pl.semaphore_signal(barrier, inc=1, device_id=at(chip(d)), device_id_type=MESH)
    pl.semaphore_signal(barrier, inc=1, device_id=sibling, device_id_type=MESH)
    for o in xs:
        pl.semaphore_signal(barrier, inc=1, device_id={"dp_0": o}, device_id_type=MESH)
    for o in zs:
        pl.semaphore_signal(barrier, inc=1, device_id={"dp_1": o}, device_id_type=MESH)

    loads = [
        pltpu.make_async_copy(src, dst, lsem.at[i])
        for i, (src, dst) in enumerate((
            (q_hbm, snd.at[0]), (k_hbm, snd.at[1]), (v_hbm, snd.at[2]), (seg_hbm, segs.at[0, y]),
            (w_hbm, w_ref), (tgt_hbm, tgt_ref)))
    ]
    for load in loads:
        load.start()

    def send(kind, slot, src, dst, to, dslot):
        return pltpu.make_async_remote_copy(
            src_ref=src, dst_ref=dst, send_sem=ssem.at[kind, slot], recv_sem=rsem.at[kind, dslot],
            device_id=to, device_id_type=MESH)

    for load in loads[:4]:
        load.wait()
    pl.semaphore_wait(barrier, 8 + len(xs) + len(zs))
    own_rows = [snd.at[:, y]]
    for d in ORDER:
        h = chip(d)
        send(0, h, snd.at[:, h], rx.at[y], at(h), y).start()
        send(1, h, segs.at[0, y], segs.at[0, y], at(h), y).start()
    send(2, y, snd.at[1:3, y], sib.at[y], sibling, y).start()
    send(3, y, segs.at[0, y], segs.at[1, y], sibling, y).start()

    id256 = eye(256)
    id128 = eye(128)
    loads[4].wait()
    loads[5].wait()
    for j in range(5):
        n = 256 if j < 4 else 128
        cols = slice(256 * j, 256 * j + n)
        unit = id256 if n == 256 else id128
        w_tr[cols, :] = mmt(unit, w_ref[:, cols]).astype(BF)
        tgt_tr[cols, :] = mmt(unit, tgt_ref[:, cols]).astype(BF)
    length = len_ref[0]

    def place(block, number, parity, source, kb, vb):
        kt[:, lanes(block, TOK)] = kb
        vt[:, lanes(block, TOK)] = vb
        rows = lanes(block, TOK)
        km[rows, :] = mmt(id128, kb).astype(BF)
        vm[rows, :] = mmt(id128, vb).astype(BF)
        at_pos = number * TOK + lax.broadcasted_iota(jnp.int32, (1, TOK), 1)
        group = jnp.where(at_pos < length, segs[parity, source], -1).astype(F32)
        spread_rows = jnp.broadcast_to(group, (TOK, TOK)).astype(BF)
        gk[rows, :] = mmt(id128, spread_rows)
        return group

    def place_own(source, qb, kb, vb):
        qt[:, lanes(source, TOK)] = qb
        gq[:, lanes(source, TOK)] = place(source, 2 * source + c, 0, source, kb, vb)

    place_own(y, snd[0, y], snd[1, y], snd[2, y])
    for d in ORDER:
        s = chip(d)
        send(0, s, snd.at[:, s], rx.at[s], at(s), s).wait_recv()
        send(1, s, segs.at[0, y], segs.at[0, s], at(s), s).wait_recv()
        send(2, s, rx.at[s, 1:3], sib.at[s], sibling, s).start()
        send(3, s, segs.at[0, s], segs.at[1, s], sibling, s).start()
        place_own(s, rx[s, 0], rx[s, 1], rx[s, 2])
    for d in (0,) + ORDER:
        s = chip(d)
        send(2, s, rx.at[s, 1:3], sib.at[s], sibling, s).wait_recv()
        send(3, s, segs.at[0, s], segs.at[1, s], sibling, s).wait_recv()
        place(8 + s, 2 * s + 1 - c, 1, s, sib[s, 0], sib[s, 1])

    scale = 1.0 / math.sqrt(HEAD_DIM)
    to_two = scale / math.log(2.0)

    def chunk(i):
        return pl.ds(pl.multiple_of(i * KCH, KCH), KCH)

    @pl.loop(0, TILES)
    def _(t):
        own_q = qt[:, lanes(t, QTILE)]
        own_g = gq[:, lanes(t, QTILE)]

        def first(i, top):
            sc = mm(km[chunk(i), :], own_q)
            g = gk[chunk(i), :]
            sc = jnp.where(jnp.concatenate([g, g], axis=1) == own_g, sc, NEG_LARGE)
            s_ref[chunk(i), :] = sc
            return jnp.maximum(top, jnp.max(sc, axis=0, keepdims=True))

        top = lax.fori_loop(0, CHUNKS, first, jnp.full((1, QTILE), NEG_LARGE, F32))

        def second(i, total):
            pr = jnp.exp2((s_ref[chunk(i), :] - top) * to_two)
            p_ref[t, chunk(i), :] = pr.astype(BF)
            return total + jnp.sum(pr, axis=0, keepdims=True)

        total = lax.fori_loop(0, CHUNKS, second, jnp.zeros((1, QTILE), F32))
        inv = 1.0 / total
        rden[t] = inv
        out = (mm(vt[...], p_ref[t]) * inv).astype(BF)
        for half in range(2):
            b = 2 * t + half
            attn_snd[b] = out[:, half * TOK:(half + 1) * TOK]

            @pl.when(b != y)
            def _():
                send(4, b, attn_snd.at[b], attn_rx.at[y], at(b), y).start()

    attn_rx[y] = attn_snd[y]
    for d in ORDER:
        s = chip(d)
        send(4, s, attn_snd.at[s], attn_rx.at[s], at(s), s).wait_recv()

    attn_t = attn_rx[...].reshape(FEAT, TOK)
    position = (2 * y + c) * TOK + lax.broadcasted_iota(jnp.int32, (1, TOK), 1)
    live = position < length
    out_t = mm(w_tr[...], attn_t)
    error = jnp.where(live, out_t - tgt_tr[...].astype(F32), 0.0)
    grad_t = (2.0 * error).astype(BF)
    gt[...] = grad_t
    go_snd[...] = mm(w_ref[...], grad_t).astype(BF).reshape(HEADS, HD, TOK)
    for d in ORDER:
        h = chip(d)
        send(5, h, go_snd.at[h], go_rx.at[y], at(h), y).start()
    send(9, 0, gt, gt_sib, sibling, 0).start()
    send(10, 0, attn_rx, attn_sib, sibling, 0).start()
    go_rx[y] = go_snd[y]

    squares = jnp.sum(error * error, axis=0, keepdims=True)
    lens = jnp.full((1, TOK), length.astype(F32), F32)
    row = lax.broadcasted_iota(jnp.int32, (8, TOK), 0)
    stats[0, 0] = jnp.where(row == 0, squares, jnp.where(row == 1, lens, 0.0))
    send(11, 0, stats.at[0, 0], stats.at[0, 1], sibling, 0).start()
    parts = []
    for h in range(HEADS):
        r = lax.broadcasted_iota(jnp.int32, (HALF_PAD, FEAT), 0)
        f = lax.broadcasted_iota(jnp.int32, (HALF_PAD, FEAT), 1)
        hit = jnp.logical_and(f - r == HD * h + HALF * c, r < HALF)
        parts.append(jnp.where(hit, 1.0, 0.0).astype(BF))
    pick = jnp.concatenate(parts, axis=0)
    send(10, 0, attn_rx, attn_sib, sibling, 0).wait_recv()
    attn_both = jnp.concatenate(
        [mm(pick, attn_t), mm(pick, attn_sib[...].reshape(FEAT, TOK))], axis=1).astype(BF)
    send(9, 0, gt, gt_sib, sibling, 0).wait_recv()
    send(11, 0, stats.at[0, 0], stats.at[0, 1], sibling, 0).wait_recv()
    stats[1, x] = stats[0, 0] + stats[0, 1]
    cx = WIDTH // nx
    cz = cx // nz
    czp = up(cz, 16)
    for o in xs + [x]:
        rows = pl.ds(pl.multiple_of(o * cx, 32), cx)
        both = jnp.concatenate([gt[rows, :], gt_sib[rows, :]], axis=1)
        x_snd[o] = mmt(both, attn_both).astype(BF)
        if o is not x:
            send(12, o, x_snd.at[o], x_rx.at[x], {"dp_0": o}, x).start()
            send(13, o, stats.at[1, x], stats.at[1, x], {"dp_0": o}, x).start()

    @pl.loop(0, TILES)
    def _(t):
        for half in range(2):
            b = 2 * t + half

            @pl.when(b != y)
            def _():
                send(5, b, go_snd.at[b], go_rx.at[b], at(b), b).wait_recv()

        both = jnp.concatenate([go_rx[2 * t], go_rx[2 * t + 1]], axis=1).astype(F32)
        scaled = (both * rden[t]).astype(BF)
        gos[t] = scaled
        attn = jnp.concatenate([attn_snd[2 * t], attn_snd[2 * t + 1]], axis=1)
        delta = jnp.sum(scaled.astype(F32) * attn.astype(F32), axis=0, keepdims=True)

        @pl.loop(0, CHUNKS)
        def _(i):
            dp = mm(vm[chunk(i), :], scaled)
            ds_ref[t, chunk(i), :] = (p_ref[t, chunk(i), :].astype(F32) * (dp - delta)).astype(BF)

        dq = (mm(kt[...], ds_ref[t]) * scale).astype(BF)
        for half in range(2):
            b = 2 * t + half
            q_snd[b] = dq[:, half * TOK:(half + 1) * TOK]

            @pl.when(b != y)
            def _():
                send(6, b, q_snd.at[b], grad_rx.at[0, y], at(b), y).start()

    def key_value(i):
        dk = jnp.zeros((HD, KCH), F32)
        dv = jnp.zeros((HD, KCH), F32)
        for t in range(TILES):
            dk = dk + mmt(qt[:, t * QTILE:(t + 1) * QTILE], ds_ref[t, chunk(i), :])
            dv = dv + mmt(gos[t], p_ref[t, chunk(i), :])
        return dk * scale, dv

    @pl.loop(0, 4)
    def _(i):
        dk, dv = key_value(i + 4)
        for half in range(2):
            b = 2 * i + half
            cols = slice(half * TOK, (half + 1) * TOK)
            xs_snd[b, 0] = dk[:, cols].astype(BF)
            xs_snd[b, 1] = dv[:, cols].astype(BF)
            send(7, b, xs_snd.at[b], xs_rx.at[b], sibling, b).start()

    @pl.loop(0, 4)
    def _(i):
        dk, dv = key_value(i)
        for half in range(2):
            b = 2 * i + half
            cols = slice(half * TOK, (half + 1) * TOK)
            send(7, b, xs_snd.at[b], xs_rx.at[b], sibling, b).wait_recv()
            kv_snd[b, 0] = (dk[:, cols] + xs_rx[b, 0].astype(F32)).astype(BF)
            kv_snd[b, 1] = (dv[:, cols] + xs_rx[b, 1].astype(F32)).astype(BF)

            @pl.when(b != y)
            def _():
                send(8, b, kv_snd.at[b], grad_rx.at[1:3, y], at(b), y).start()

    grad_rx[0, y] = q_snd[y]
    grad_rx[1, y] = kv_snd[y, 0]
    grad_rx[2, y] = kv_snd[y, 1]

    for o in xs:
        send(12, o, x_snd.at[o], x_rx.at[o], {"dp_0": o}, o).wait_recv()
        send(13, o, stats.at[1, x], stats.at[1, o], {"dp_0": o}, o).wait_recv()
    acc = x_snd[x].astype(F32)
    tot = stats[1, x]
    for o in xs:
        acc = acc + x_rx[o].astype(F32)
        tot = tot + stats[1, o]
    x_sum[...] = acc
    stats[2, z] = tot
    for k in range(nz):
        z_snd[k, 0:cz] = x_sum[k * cz:(k + 1) * cz, :].astype(BF)
        if czp > cz:
            z_snd[k, cz:czp] = jnp.zeros((czp - cz, LANES), BF)
    for o in zs:
        send(14, o, z_snd.at[o], z_rx.at[z], {"dp_1": o}, z).start()
        send(15, o, stats.at[2, z], stats.at[2, z], {"dp_1": o}, z).start()

    for d in ORDER:
        s = chip(d)
        send(6, s, q_snd.at[s], grad_rx.at[0, s], at(s), s).wait_recv()
    for o in zs:
        send(14, o, z_snd.at[o], z_rx.at[o], {"dp_1": o}, o).wait_recv()
        send(15, o, stats.at[2, z], stats.at[2, o], {"dp_1": o}, o).wait_recv()
    acc = z_snd[z].astype(F32)
    tot = stats[2, z]
    for o in zs:
        acc = acc + z_rx[o].astype(F32)
        tot = tot + stats[2, o]
    stats[3, y] = tot
    turned = mmt(eye(LANES), acc.astype(BF)).astype(BF)
    y_snd[:, :, 0:czp] = turned.reshape(HEADS, HALF_PAD, czp)
    for d in ORDER:
        h = chip(d)
        send(16, h, y_snd.at[h], y_rx.at[y], at(h), y).start()
        send(17, h, stats.at[3, y], stats.at[3, y], at(h), y).start()
    y_rx[y] = y_snd[y]
    for d in ORDER:
        s = chip(d)
        send(8, s, kv_snd.at[s], grad_rx.at[1:3, s], at(s), s).wait_recv()
        send(16, s, y_snd.at[s], y_rx.at[s], at(s), s).wait_recv()
        send(17, s, stats.at[3, y], stats.at[3, s], at(s), s).wait_recv()
    tot = jnp.zeros((8, TOK), F32)
    acc = jnp.zeros((HALF_PAD, czp), F32)
    for s in range(8):
        tot = tot + stats[3, s]
        acc = acc + y_rx[s, :, 0:czp].astype(F32)
    stat_ref[...] = tot
    wg_ref[...] = acc[0:HALF, 0:cz]
    ratio = jnp.float32(16 * TOK * 16 * nx * nz) / tot[1:2]
    for j, ref in enumerate((dq_ref, dk_ref, dv_ref)):
        ref[...] = grad_rx[j].reshape(FEAT, TOK).astype(F32) * ratio

    for d in (0,) + ORDER:
        s = chip(d)
        if d:
            send(0, s, snd.at[:, s], rx.at[y], at(s), y).wait_send()
            send(1, s, segs.at[0, y], segs.at[0, y], at(s), y).wait_send()
            send(4, s, attn_snd.at[s], attn_rx.at[y], at(s), y).wait_send()
            send(5, s, go_snd.at[s], go_rx.at[y], at(s), y).wait_send()
            send(6, s, q_snd.at[s], grad_rx.at[0, y], at(s), y).wait_send()
            send(8, s, kv_snd.at[s], grad_rx.at[1:3, y], at(s), y).wait_send()
            send(16, s, y_snd.at[s], y_rx.at[y], at(s), y).wait_send()
            send(17, s, stats.at[3, y], stats.at[3, y], at(s), y).wait_send()
        send(2, s, rx.at[s, 1:3], sib.at[s], sibling, s).wait_send()
        send(3, s, segs.at[0, s], segs.at[1, s], sibling, s).wait_send()
        send(7, s, xs_snd.at[s], xs_rx.at[s], sibling, s).wait_send()
    send(9, 0, gt, gt_sib, sibling, 0).wait_send()
    send(10, 0, attn_rx, attn_sib, sibling, 0).wait_send()
    send(11, 0, stats.at[0, 0], stats.at[0, 1], sibling, 0).wait_send()
    for o in xs:
        send(12, o, x_snd.at[o], x_rx.at[x], {"dp_0": o}, x).wait_send()
        send(13, o, stats.at[1, x], stats.at[1, x], {"dp_0": o}, x).wait_send()
    for o in zs:
        send(14, o, z_snd.at[o], z_rx.at[z], {"dp_1": o}, z).wait_send()
        send(15, o, stats.at[2, z], stats.at[2, z], {"dp_1": o}, z).wait_send()


def attention(q, k, v, w, target, lengths, segments):
    vm = pltpu.VMEM
    vmem = pl.BlockSpec(memory_space=pltpu.VMEM)
    hbm = pl.BlockSpec(memory_space=pl.ANY)
    keys = 16 * TOK
    nx = lax.axis_size("dp_0")
    nz = lax.axis_size("dp_1")
    cx = WIDTH // nx
    cz = cx // nz
    czp = up(cz, 16)
    HD = HEAD_DIM
    heads_of = lambda n: vm((HEADS, HD, TOK) if n is None else (HEADS, n, HD, TOK), BF)
    return pl.pallas_call(
        kernel,
        out_shape=[jax.ShapeDtypeStruct((FEAT, TOK), F32)] * 3 + [
            jax.ShapeDtypeStruct((HALF, cz), F32),
            jax.ShapeDtypeStruct((8, TOK), F32),
        ],
        in_specs=[hbm] * 5 + [pl.BlockSpec(memory_space=pltpu.SMEM), hbm],
        out_specs=[vmem] * 5,
        scratch_shapes=[
            vm((3, HEADS, HD, TOK), BF),
            vm((FEAT, WIDTH), BF),
            vm((TOK, WIDTH), BF),
            heads_of(3),
            heads_of(2),
            vm((2, HEADS, 1, TOK), jnp.int32),
            vm((HD, 8 * TOK), BF),
            vm((HD, keys), BF),
            vm((HD, keys), BF),
            vm((keys, HD), BF),
            vm((keys, HD), BF),
            vm((keys, TOK), F32),
            vm((1, 8 * TOK), F32),
            vm((keys, QTILE), F32),
            vm((TILES, keys, QTILE), BF),
            vm((TILES, keys, QTILE), BF),
            vm((TILES, 1, QTILE), F32),
            vm((WIDTH, FEAT), BF),
            vm((WIDTH, TOK), BF),
            heads_of(None),
            heads_of(None),
            heads_of(None),
            heads_of(None),
            vm((TILES, HD, QTILE), BF),
            heads_of(None),
            heads_of(2),
            heads_of(2),
            heads_of(2),
            vm((3, HEADS, HD, TOK), BF),
            vm((WIDTH, TOK), BF),
            vm((WIDTH, TOK), BF),
            heads_of(None),
            vm((4, 8, 8, TOK), F32),
            vm((nx, cx, LANES), BF),
            vm((nx, cx, LANES), BF),
            vm((cx, LANES), F32),
            vm((nz, czp, LANES), BF),
            vm((nz, czp, LANES), BF),
            vm((HEADS, HALF_PAD, up(czp, 128)), BF),
            vm((HEADS, HALF_PAD, up(czp, 128)), BF),
            pltpu.SemaphoreType.DMA((6,)),
            pltpu.SemaphoreType.DMA((18, 8)),
            pltpu.SemaphoreType.DMA((18, 8)),
        ],
        compiler_params=pltpu.CompilerParams(
            collective_id=0, has_side_effects=True, vmem_limit_bytes=62 * 1024 * 1024),
        name="attention",
    )(q, k, v, w, target, lengths, segments)


def local(query_rows, key_rows, value_rows, out_weight, target, lengths, segments):
    groups = lax.axis_size(DP)
    total_rows = TOK * lax.axis_size(PATCH)
    by_head = lambda rows: rows[0].T.reshape(HEADS, HEAD_DIM, TOK)
    dq, dk, dv, weight, stats = attention(
        by_head(query_rows), by_head(key_rows), by_head(value_rows), out_weight, target[0],
        lengths, segments)
    count = stats[1, 0] / lax.axis_size(PATCH)
    ratio = jnp.float32(groups * total_rows) / count
    loss = jnp.sum(stats[0]) / (count * WIDTH)
    return (dq.T[None], dk.T[None], dv.T[None], weight * (ratio / total_rows), loss)


def solution(mesh):
    torus = Mesh(mesh.devices.reshape(4, 8, 8, 2), ("dp_0", "dp_1", "patch_0", "patch_1"))
    return jax.shard_map(
        local,
        mesh=torus,
        in_specs=(P(DP, PATCH, None), P(DP, PATCH, None), P(DP, PATCH, None), P(),
                  P(DP, PATCH, None), P(DP), P(DP, PATCH)),
        out_specs=(P(DP, PATCH, None), P(DP, PATCH, None), P(DP, PATCH, None), P(PATCH, DP), P()),
        check_vma=False,
    )
```

time: 164 us -> 89 us (0.54)
  waiting for transfers between devices: 54.6 us -> 0 us
  starting transfers between devices: 31.6 us -> 0 us
  Pallas kernels: 55.3 us -> 76.3 us
  local copies, waits for them, and re-layouts: 14.2 us -> 5.33 us
    all_to_all x4 -> x0, waiting for transfers between devices: 54.6 us -> none  [the longest x2 40.8 us: sum_at_owner(): lax.all_to_all(in_blocks(value, dim, peers), axis, 0, 0, tiled=True)]
    all_to_all x4 -> x0, starting transfers between devices: 31.6 us -> none  [the longest x2 22.2 us: from_everyone(): return lax.all_to_all(copies, axis, split_axis=0, concat_axis=0, tiled=True)]
    pallas_call x1, Pallas kernels: 55.3 us -> 76.3 us  [attention(): pl.pallas_call(kernel, out_shape=[jax.ShapeDtypeStruct((FEAT, TOK), F32)]...]
    unnamed x14 -> x5, local copies, waits for them, and re-layouts: 10.1 us -> 4.1 us
    reshape x2 -> x0, local copies, waits for them, and re-layouts: 2.07 us -> none  [in_blocks(): value.reshape(*shape[:dim], peers, shape[dim] // peers, *shape[dim + 1:])]
  transfers between devices with their start and end apart: 4 -> 0, of which waited for: 4 -> 0; matrix products, arithmetic and copies ran while one was open for 3% -> 0% of each run, Pallas kernels for 0% -> 0%
where the time goes in v2:
time: 89 us; the launch traced here: 88.7 us
  Pallas kernels  76.3 us (86%)
  local copies, waits for them, and re-layouts  5.33 us (6%)
  between operations  4.43 us (5%)
  other arithmetic  2.61 us (3%)
    pallas_call x1, Pallas kernels, attention(): pl.pallas_call(kernel, out_shape=[jax.ShapeDtypeStruct((FEAT, TOK), F32)]...  76.3 us
    unnamed x5, local copies, waits for them, and re-layouts  4.1 us

profile of v2, /device:TPU:1, one launch (start us, length us, event | category | flops | bytes accessed | tf_op | source)
XLA Modules:
  0.0 88.7 jit_solution(15251789805081704852)
XLA Ops:
  1.3 76.3 %attention.1 = (f32[576,128]{1,0:T(8,128)}, f32[576,128]{1,0:T(8,128)}, f32[576,128]{1,0:T(8,128)}, f32[36,36]{1,0:T(8,128)}, f32[8,128]{1,0:T(8,128)}) custom-call(bf16[8,72,128]{2,1,0:T(8,128)(2,1)} %bitcast.31, bf16[8,72,128]{2,1,0:T(8,128)(2,1)} %bitcast.32, bf16[8,72,128]{2,1,0:T(8,128)(2,1)} %bitcast.33, bf16[576,1152]{1,0:T(8,128)(2,1)} %w_hbm.1, ...), custom_call_target="tpu_custom_call" | custom-call | tf_op jit(solution)/shard_map/attention/pallas_call | solution.py:392
  77.6 0.0 copy-start
  77.6 1.2 %slice.6 = f32[1,1]{1,0:T(1,128)} slice(f32[8,128]{1,0:T(8,128)} %get-tuple-element.14), slice={[1:2], [0:1]} | slice | bytes 8 | tf_op jit(solution)/shard_map/slice | solution.py:458
  79.5 1.3 %slice_reduce_fusion = f32[]{:T(128)} fusion(f32[8,128]{1,0:T(8,128)} %get-tuple-element.14), kind=kLoop, calls=%fused_computation.1 | loop fusion | flops 127 | bytes 516 | tf_op jit(solution)/shard_map/reduce_sum | solution.py:460
  82.1 1.3 %broadcast_multiply_fusion = f32[36,36]{1,0:T(8,128)} fusion(f32[36,36]{1,0:T(8,128)} %get-tuple-element.13, f32[]{:T(128)} %bitcast.16), kind=kLoop, calls=%fused_computation | loop fusion | flops 1296 | bytes 10372 | tf_op jit(solution)/shard_map/mul | solution.py:461
  83.4 1.7 %copy.16 = f32[1,128,576]{1,2,0:T(8,128)} copy(f32[1,128,576]{1,2,0:T(8,128)} %bitcast.30) | data formatting | bytes 589824
  85.1 1.7 %copy.17 = f32[1,128,576]{1,2,0:T(8,128)} copy(f32[1,128,576]{1,2,0:T(8,128)} %bitcast.29) | data formatting | bytes 589824
  86.8 0.0 copy-done
  86.8 0.7 copy.18
Async XLA Ops:
  77.6 9.2 %copy-start = (f32[576,128]{1,0:T(8,128)S(1)}, f32[576,128]{1,0:T(8,128)}, u32[]{:S(2)}) copy-start(f32[576,128]{1,0:T(8,128)} %get-tuple-element.12) | copy-start | bytes 884740

commit v3 on v2

--- a/solution.py
+++ b/solution.py
@@ -26,6 +26,8 @@
 ORDER = (4, 3, 5, 2, 6, 1, 7)
 QTILE = 256
 TILES = 4
+FAR_FIRST = (2, 1, 3, 0)
+NEAR_FIRST = (0, 1, 3, 2)
 KCH = 256
 CHUNKS = 8
 
@@ -54,9 +56,9 @@
 
 def kernel(
     q_hbm, k_hbm, v_hbm, w_hbm, tgt_hbm, len_ref, seg_hbm,
-    dq_ref, dk_ref, dv_ref, wg_ref, stat_ref,
+    grad_rx, wg_ref, stat_ref,
     snd, w_ref, tgt_ref, rx, sib, segs, qt, kt, vt, km, vm, gk, gq, s_ref, p_ref, ds_ref, rden,
-    w_tr, tgt_tr, attn_snd, attn_rx, go_snd, go_rx, gos, q_snd, xs_snd, xs_rx, kv_snd, grad_rx,
+    w_tr, tgt_tr, attn_snd, attn_rx, go_snd, go_rx, gos, q_snd, xs_snd, xs_rx, kv_snd,
     gt, gt_sib, attn_sib, stats, x_snd, x_rx, x_sum, z_snd, z_rx, y_snd, y_rx,
     lsem, ssem, rsem,
 ):
@@ -134,7 +136,13 @@
         qt[:, lanes(source, TOK)] = qb
         gq[:, lanes(source, TOK)] = place(source, 2 * source + c, 0, source, kb, vb)
 
+    def place_sibling(source):
+        send(2, source, rx.at[source, 1:3], sib.at[source], sibling, source).wait_recv()
+        send(3, source, segs.at[0, source], segs.at[1, source], sibling, source).wait_recv()
+        place(8 + source, 2 * source + 1 - c, 1, source, sib[source, 0], sib[source, 1])
+
     place_own(y, snd[0, y], snd[1, y], snd[2, y])
+    before = y
     for d in ORDER:
         s = chip(d)
         send(0, s, snd.at[:, s], rx.at[s], at(s), s).wait_recv()
@@ -142,11 +150,9 @@
         send(2, s, rx.at[s, 1:3], sib.at[s], sibling, s).start()
         send(3, s, segs.at[0, s], segs.at[1, s], sibling, s).start()
         place_own(s, rx[s, 0], rx[s, 1], rx[s, 2])
-    for d in (0,) + ORDER:
-        s = chip(d)
-        send(2, s, rx.at[s, 1:3], sib.at[s], sibling, s).wait_recv()
-        send(3, s, segs.at[0, s], segs.at[1, s], sibling, s).wait_recv()
-        place(8 + s, 2 * s + 1 - c, 1, s, sib[s, 0], sib[s, 1])
+        place_sibling(before)
+        before = s
+    place_sibling(before)
 
     scale = 1.0 / math.sqrt(HEAD_DIM)
     to_two = scale / math.log(2.0)
@@ -154,27 +160,40 @@
     def chunk(i):
         return pl.ds(pl.multiple_of(i * KCH, KCH), KCH)
 
+    pair = y // 2
+
+    def nth(order, n):
+        first = jnp.where(n == 0, order[0], jnp.where(n == 1, order[1], jnp.where(n == 2, order[2], order[3])))
+        return lax.rem(pair + first, TILES)
+
+    def fold(v, op):
+        n = v.shape[0] // 8
+        parts = [v[8 * i:8 * i + 8] for i in range(n)]
+        while len(parts) > 1:
+            parts = [op(*parts[i:i + 2]) if i + 1 < len(parts) else parts[i] for i in range(0, len(parts), 2)]
+        return parts[0]
+
     @pl.loop(0, TILES)
-    def _(t):
+    def _(n):
+        t = nth(FAR_FIRST, n)
         own_q = qt[:, lanes(t, QTILE)]
         own_g = gq[:, lanes(t, QTILE)]
-
-        def first(i, top):
-            sc = mm(km[chunk(i), :], own_q)
-            g = gk[chunk(i), :]
+        top = jnp.full((8, QTILE), NEG_LARGE, F32)
+        for i in range(CHUNKS):
+            part = slice(i * KCH, (i + 1) * KCH)
+            sc = mm(km[part, :], own_q)
+            g = gk[part, :]
             sc = jnp.where(jnp.concatenate([g, g], axis=1) == own_g, sc, NEG_LARGE)
-            s_ref[chunk(i), :] = sc
-            return jnp.maximum(top, jnp.max(sc, axis=0, keepdims=True))
-
-        top = lax.fori_loop(0, CHUNKS, first, jnp.full((1, QTILE), NEG_LARGE, F32))
-
-        def second(i, total):
-            pr = jnp.exp2((s_ref[chunk(i), :] - top) * to_two)
-            p_ref[t, chunk(i), :] = pr.astype(BF)
-            return total + jnp.sum(pr, axis=0, keepdims=True)
-
-        total = lax.fori_loop(0, CHUNKS, second, jnp.zeros((1, QTILE), F32))
-        inv = 1.0 / total
+            s_ref[part, :] = sc
+            top = jnp.maximum(top, fold(sc, jnp.maximum))
+        top = jnp.max(top, axis=0, keepdims=True)
+        total = jnp.zeros((8, QTILE), F32)
+        for i in range(CHUNKS):
+            part = slice(i * KCH, (i + 1) * KCH)
+            pr = jnp.exp2((s_ref[part, :] - top) * to_two)
+            p_ref[t, part, :] = pr.astype(BF)
+            total = total + fold(pr, jnp.add)
+        inv = 1.0 / jnp.sum(total, axis=0, keepdims=True)
         rden[t] = inv
         out = (mm(vt[...], p_ref[t]) * inv).astype(BF)
         for half in range(2):
@@ -190,6 +209,7 @@
         s = chip(d)
         send(4, s, attn_snd.at[s], attn_rx.at[s], at(s), s).wait_recv()
 
+    send(10, 0, attn_rx, attn_sib, sibling, 0).start()
     attn_t = attn_rx[...].reshape(FEAT, TOK)
     position = (2 * y + c) * TOK + lax.broadcasted_iota(jnp.int32, (1, TOK), 1)
     live = position < length
@@ -197,19 +217,18 @@
     error = jnp.where(live, out_t - tgt_tr[...].astype(F32), 0.0)
     grad_t = (2.0 * error).astype(BF)
     gt[...] = grad_t
-    go_snd[...] = mm(w_ref[...], grad_t).astype(BF).reshape(HEADS, HD, TOK)
-    for d in ORDER:
-        h = chip(d)
-        send(5, h, go_snd.at[h], go_rx.at[y], at(h), y).start()
-    send(9, 0, gt, gt_sib, sibling, 0).start()
-    send(10, 0, attn_rx, attn_sib, sibling, 0).start()
-    go_rx[y] = go_snd[y]
-
-    squares = jnp.sum(error * error, axis=0, keepdims=True)
+    squares = jnp.sum(fold(error * error, jnp.add), axis=0, keepdims=True)
     lens = jnp.full((1, TOK), length.astype(F32), F32)
     row = lax.broadcasted_iota(jnp.int32, (8, TOK), 0)
     stats[0, 0] = jnp.where(row == 0, squares, jnp.where(row == 1, lens, 0.0))
+    send(9, 0, gt, gt_sib, sibling, 0).start()
     send(11, 0, stats.at[0, 0], stats.at[0, 1], sibling, 0).start()
+    go_snd[...] = mm(w_ref[...], grad_t).astype(BF).reshape(HEADS, HD, TOK)
+    for d in ORDER:
+        h = chip(d)
+        send(5, h, go_snd.at[h], go_rx.at[y], at(h), y).start()
+    go_rx[y] = go_snd[y]
+
     parts = []
     for h in range(HEADS):
         r = lax.broadcasted_iota(jnp.int32, (HALF_PAD, FEAT), 0)
@@ -225,17 +244,38 @@
     stats[1, x] = stats[0, 0] + stats[0, 1]
     cx = WIDTH // nx
     cz = cx // nz
-    czp = up(cz, 16)
-    for o in xs + [x]:
-        rows = pl.ds(pl.multiple_of(o * cx, 32), cx)
-        both = jnp.concatenate([gt[rows, :], gt_sib[rows, :]], axis=1)
-        x_snd[o] = mmt(both, attn_both).astype(BF)
-        if o is not x:
-            send(12, o, x_snd.at[o], x_rx.at[x], {"dp_0": o}, x).start()
-            send(13, o, stats.at[1, x], stats.at[1, x], {"dp_0": o}, x).start()
+    czp = up(cz, 8)
+    ch = cx // 2
+    for half in range(2):
+        for o in xs + [x]:
+            rows = pl.ds(pl.multiple_of(o * cx + half * ch, 16), ch)
+            both = jnp.concatenate([gt[rows, :], gt_sib[rows, :]], axis=1)
+            x_snd[half, o] = mmt(both, attn_both).astype(BF)
+            if o is not x:
+                send(12 + half, o, x_snd.at[half, o], x_rx.at[half, x], {"dp_0": o}, x).start()
+                if half == 0:
+                    send(18, o, stats.at[1, x], stats.at[1, x], {"dp_0": o}, x).start()
+
+    def sum_over_x(half):
+        for o in xs:
+            send(12 + half, o, x_snd.at[half, o], x_rx.at[half, o], {"dp_0": o}, o).wait_recv()
+        acc = x_snd[half, x].astype(F32)
+        for o in xs:
+            acc = acc + x_rx[half, o].astype(F32)
+        x_sum[half] = acc
+        for k in range(nz // 2):
+            to = half * (nz // 2) + k
+            z_snd[to, 0:cz] = x_sum[half, k * cz:(k + 1) * cz, :].astype(BF)
+            if czp > cz:
+                z_snd[to, cz:czp] = jnp.zeros((czp - cz, LANES), BF)
+
+            @pl.when(to != z)
+            def _():
+                send(14, to, z_snd.at[to], z_rx.at[z], {"dp_1": to}, z).start()
 
     @pl.loop(0, TILES)
-    def _(t):
+    def _(n):
+        t = nth(NEAR_FIRST, n)
         for half in range(2):
             b = 2 * t + half
 
@@ -248,12 +288,10 @@
         gos[t] = scaled
         attn = jnp.concatenate([attn_snd[2 * t], attn_snd[2 * t + 1]], axis=1)
         delta = jnp.sum(scaled.astype(F32) * attn.astype(F32), axis=0, keepdims=True)
-
-        @pl.loop(0, CHUNKS)
-        def _(i):
-            dp = mm(vm[chunk(i), :], scaled)
-            ds_ref[t, chunk(i), :] = (p_ref[t, chunk(i), :].astype(F32) * (dp - delta)).astype(BF)
-
+        for i in range(CHUNKS):
+            part = slice(i * KCH, (i + 1) * KCH)
+            dp = mm(vm[part, :], scaled)
+            ds_ref[t, part, :] = (p_ref[t, part, :].astype(F32) * (dp - delta)).astype(BF)
         dq = (mm(kt[...], ds_ref[t]) * scale).astype(BF)
         for half in range(2):
             b = 2 * t + half
@@ -271,8 +309,8 @@
             dv = dv + mmt(gos[t], p_ref[t, chunk(i), :])
         return dk * scale, dv
 
-    @pl.loop(0, 4)
-    def _(i):
+    for n in range(4):
+        i = nth(FAR_FIRST, n)
         dk, dv = key_value(i + 4)
         for half in range(2):
             b = 2 * i + half
@@ -281,8 +319,9 @@
             xs_snd[b, 1] = dv[:, cols].astype(BF)
             send(7, b, xs_snd.at[b], xs_rx.at[b], sibling, b).start()
 
-    @pl.loop(0, 4)
-    def _(i):
+    sum_over_x(0)
+    for n in range(4):
+        i = nth(FAR_FIRST, n)
         dk, dv = key_value(i)
         for half in range(2):
             b = 2 * i + half
@@ -299,22 +338,13 @@
     grad_rx[1, y] = kv_snd[y, 0]
     grad_rx[2, y] = kv_snd[y, 1]
 
-    for o in xs:
-        send(12, o, x_snd.at[o], x_rx.at[o], {"dp_0": o}, o).wait_recv()
-        send(13, o, stats.at[1, x], stats.at[1, o], {"dp_0": o}, o).wait_recv()
-    acc = x_snd[x].astype(F32)
+    sum_over_x(1)
     tot = stats[1, x]
     for o in xs:
-        acc = acc + x_rx[o].astype(F32)
+        send(18, o, stats.at[1, x], stats.at[1, o], {"dp_0": o}, o).wait_recv()
         tot = tot + stats[1, o]
-    x_sum[...] = acc
     stats[2, z] = tot
-    for k in range(nz):
-        z_snd[k, 0:cz] = x_sum[k * cz:(k + 1) * cz, :].astype(BF)
-        if czp > cz:
-            z_snd[k, cz:czp] = jnp.zeros((czp - cz, LANES), BF)
     for o in zs:
-        send(14, o, z_snd.at[o], z_rx.at[z], {"dp_1": o}, z).start()
         send(15, o, stats.at[2, z], stats.at[2, z], {"dp_1": o}, z).start()
 
     for d in ORDER:
@@ -348,9 +378,6 @@
         acc = acc + y_rx[s, :, 0:czp].astype(F32)
     stat_ref[...] = tot
     wg_ref[...] = acc[0:HALF, 0:cz]
-    ratio = jnp.float32(16 * TOK * 16 * nx * nz) / tot[1:2]
-    for j, ref in enumerate((dq_ref, dk_ref, dv_ref)):
-        ref[...] = grad_rx[j].reshape(FEAT, TOK).astype(F32) * ratio
 
     for d in (0,) + ORDER:
         s = chip(d)
@@ -370,8 +397,9 @@
     send(10, 0, attn_rx, attn_sib, sibling, 0).wait_send()
     send(11, 0, stats.at[0, 0], stats.at[0, 1], sibling, 0).wait_send()
     for o in xs:
-        send(12, o, x_snd.at[o], x_rx.at[x], {"dp_0": o}, x).wait_send()
-        send(13, o, stats.at[1, x], stats.at[1, x], {"dp_0": o}, x).wait_send()
+        send(12, o, x_snd.at[0, o], x_rx.at[0, x], {"dp_0": o}, x).wait_send()
+        send(13, o, x_snd.at[1, o], x_rx.at[1, x], {"dp_0": o}, x).wait_send()
+        send(18, o, stats.at[1, x], stats.at[1, x], {"dp_0": o}, x).wait_send()
     for o in zs:
         send(14, o, z_snd.at[o], z_rx.at[z], {"dp_1": o}, z).wait_send()
         send(15, o, stats.at[2, z], stats.at[2, z], {"dp_1": o}, z).wait_send()
@@ -380,23 +408,24 @@
 def attention(q, k, v, w, target, lengths, segments):
     vm = pltpu.VMEM
     vmem = pl.BlockSpec(memory_space=pltpu.VMEM)
-    hbm = pl.BlockSpec(memory_space=pl.ANY)
+    hbm = pl.BlockSpec(memory_space=pltpu.HBM)
     keys = 16 * TOK
     nx = lax.axis_size("dp_0")
     nz = lax.axis_size("dp_1")
     cx = WIDTH // nx
     cz = cx // nz
-    czp = up(cz, 16)
+    czp = up(cz, 8)
     HD = HEAD_DIM
     heads_of = lambda n: vm((HEADS, HD, TOK) if n is None else (HEADS, n, HD, TOK), BF)
     return pl.pallas_call(
         kernel,
-        out_shape=[jax.ShapeDtypeStruct((FEAT, TOK), F32)] * 3 + [
+        out_shape=[
+            jax.ShapeDtypeStruct((3, HEADS, HD, TOK), BF),
             jax.ShapeDtypeStruct((HALF, cz), F32),
             jax.ShapeDtypeStruct((8, TOK), F32),
         ],
         in_specs=[hbm] * 5 + [pl.BlockSpec(memory_space=pltpu.SMEM), hbm],
-        out_specs=[vmem] * 5,
+        out_specs=[vmem] * 3,
         scratch_shapes=[
             vm((3, HEADS, HD, TOK), BF),
             vm((FEAT, WIDTH), BF),
@@ -426,39 +455,55 @@
             heads_of(2),
             heads_of(2),
             heads_of(2),
-            vm((3, HEADS, HD, TOK), BF),
             vm((WIDTH, TOK), BF),
             vm((WIDTH, TOK), BF),
             heads_of(None),
             vm((4, 8, 8, TOK), F32),
-            vm((nx, cx, LANES), BF),
-            vm((nx, cx, LANES), BF),
-            vm((cx, LANES), F32),
+            vm((2, nx, cx // 2, LANES), BF),
+            vm((2, nx, cx // 2, LANES), BF),
+            vm((2, cx // 2, LANES), F32),
             vm((nz, czp, LANES), BF),
             vm((nz, czp, LANES), BF),
             vm((HEADS, HALF_PAD, up(czp, 128)), BF),
             vm((HEADS, HALF_PAD, up(czp, 128)), BF),
             pltpu.SemaphoreType.DMA((6,)),
-            pltpu.SemaphoreType.DMA((18, 8)),
-            pltpu.SemaphoreType.DMA((18, 8)),
+            pltpu.SemaphoreType.DMA((19, 8)),
+            pltpu.SemaphoreType.DMA((19, 8)),
         ],
         compiler_params=pltpu.CompilerParams(
-            collective_id=0, has_side_effects=True, vmem_limit_bytes=62 * 1024 * 1024),
+            collective_id=0, has_side_effects=True, vmem_limit_bytes=40 * 1024 * 1024),
         name="attention",
     )(q, k, v, w, target, lengths, segments)
 
 
+def finish(grads, part, stats, dq_ref, dk_ref, dv_ref, wg_ref, loss_ref):
+    slots = 16 * TOK
+    packs = lax.axis_size("dp_0") * lax.axis_size("dp_1")
+    lens = stats[1:2]
+    ratio = jnp.float32(slots * 16 * packs) / lens
+    loss_ref[...] = jnp.sum(stats[0:1] / (lens * (WIDTH / 16)), axis=1, keepdims=True)
+    wg_ref[...] = part[...] * (ratio[:, 0:1] * (1.0 / slots))
+    for j, ref in enumerate((dq_ref, dk_ref, dv_ref)):
+        ref[...] = grads[j].reshape(FEAT, TOK).astype(F32) * ratio
+
+
 def local(query_rows, key_rows, value_rows, out_weight, target, lengths, segments):
-    groups = lax.axis_size(DP)
-    total_rows = TOK * lax.axis_size(PATCH)
-    by_head = lambda rows: rows[0].T.reshape(HEADS, HEAD_DIM, TOK)
-    dq, dk, dv, weight, stats = attention(
-        by_head(query_rows), by_head(key_rows), by_head(value_rows), out_weight, target[0],
-        lengths, segments)
-    count = stats[1, 0] / lax.axis_size(PATCH)
-    ratio = jnp.float32(groups * total_rows) / count
-    loss = jnp.sum(stats[0]) / (count * WIDTH)
-    return (dq.T[None], dk.T[None], dv.T[None], weight * (ratio / total_rows), loss)
+    stay = lambda value: pltpu.with_memory_space_constraint(value, pltpu.HBM)
+    by_head = lambda rows: stay(rows[0].T.reshape(HEADS, HEAD_DIM, TOK))
+    grads, part, stats = attention(
+        by_head(query_rows), by_head(key_rows), by_head(value_rows), stay(out_weight),
+        stay(target[0]), lengths, stay(segments))
+    vmem = pl.BlockSpec(memory_space=pltpu.VMEM)
+    dq, dk, dv, weight, loss = pl.pallas_call(
+        finish,
+        out_shape=[jax.ShapeDtypeStruct((FEAT, TOK), F32)] * 3 + [
+            jax.ShapeDtypeStruct(part.shape, F32), jax.ShapeDtypeStruct((1, 1), F32)],
+        in_specs=[vmem] * 3,
+        out_specs=[vmem] * 5,
+        compiler_params=pltpu.CompilerParams(vmem_limit_bytes=8 * 1024 * 1024),
+        name="finish",
+    )(grads, part, stats)
+    return (dq.T[None], dk.T[None], dv.T[None], weight, loss.reshape(()))
 
 
 def solution(mesh):

time: 89 us -> 68.1 us (0.77)
  Pallas kernels: 76.3 us -> 66.4 us
  local copies, waits for them, and re-layouts: 5.33 us -> 0 us
  between operations: 4.43 us -> 1.29 us
  other arithmetic: 2.61 us -> 0 us
    pallas_call x1 -> x2, Pallas kernels: 76.3 us -> 66.4 us  [the longest x1 65.5 us: attention(): pl.pallas_call(kernel, out_shape=[jax.ShapeDtypeStruct((3, HEADS, HD, TOK...]
    unnamed x5 -> x0, local copies, waits for them, and re-layouts: 4.1 us -> none
    mul x1 -> x0, other arithmetic: 1.34 us -> none  [local(): weight * (ratio / total_rows)]
    reduce_sum x1 -> x0, other arithmetic: 1.28 us -> none  [local(): loss = jnp.sum(stats[0]) / (count * WIDTH)]
    slice x1 -> x0, local copies, waits for them, and re-layouts: 1.23 us -> none  [local(): count = stats[1, 0] / lax.axis_size(PATCH)]
where the time goes in v3:
time: 68.1 us; the launch traced here: 67.7 us
  Pallas kernels  66.4 us (98%)
  between operations  1.29 us (2%)
    pallas_call x1, Pallas kernels, attention(): pl.pallas_call(kernel, out_shape=[jax.ShapeDtypeStruct((3, HEADS, HD, TOK...  65.5 us

profile of v3, /device:TPU:1, one launch (start us, length us, event | category | flops | bytes accessed | tf_op | source)
XLA Modules:
  0.0 67.7 jit_solution(12974729725354910049)
XLA Ops:
  1.3 65.5 %attention.1 = (bf16[3,8,72,128]{3,2,1,0:T(8,128)(2,1)S(1)}, f32[36,36]{1,0:T(8,128)S(1)}, f32[8,128]{1,0:T(8,128)S(1)}) custom-call(bf16[8,72,128]{2,1,0:T(8,128)(2,1)} %bitcast.27, bf16[8,72,128]{2,1,0:T(8,128)(2,1)} %bitcast.28, bf16[8,72,128]{2,1,0:T(8,128)(2,1)} %bitcast.29, bf16[576,1152]{1,0:T(8,128)(2,1)} %w_hbm.1, bf16[128,1152]{1,0:T(8,128)(2,1)} %bitcast.26, ...), custom_call_target="tpu_custom_call" | custom-call | tf_op jit(solution)/shard_map/attention/pallas_call | solution.py:420
  66.8 0.9 %finish.1 = (f32[576,128]{1,0:T(8,128)}, f32[576,128]{1,0:T(8,128)}, f32[576,128]{1,0:T(8,128)}, f32[36,36]{1,0:T(8,128)}, f32[1,1]{1,0:T(1,128)}) custom-call(bf16[3,8,72,128]{3,2,1,0:T(8,128)(2,1)S(1)} %get-tuple-element.13.grads, f32[36,36]{1,0:T(8,128)S(1)} %get-tuple-element.14.part, f32[8,128]{1,0:T(8,128)S(1)} %get-tuple-element.15.stats), custom_call_target="tpu_custom_call" | custom-call | tf_op jit(solution)/shard_map/finish/pallas_call | solution.py:497

commit v4 on v3

v4 whole, which is shorter than its diff:
```python
import math

import jax
import jax.numpy as jnp
from jax import lax
from jax.experimental import pallas as pl
from jax.experimental.pallas import tpu as pltpu
from jax.sharding import Mesh
from jax.sharding import PartitionSpec as P

WIDTH = 1152
HEADS = 8
HEAD_DIM = 72
FEAT = 576
TOK = 128
HALF = 36
HALF_PAD = 48
LANES = HEADS * HALF_PAD
PATCH = ("patch_0", "patch_1")
DP = ("dp_0", "dp_1")
DP_PATCH = ("dp_0", "dp_1", "patch_0", "patch_1")
NEG_LARGE = -1e30
MESH = pl.DeviceIdType.MESH
BF = jnp.bfloat16
F32 = jnp.float32
ORDER = (4, 3, 5, 2, 6, 1, 7)
QTILE = 256
TILES = 4
SLOTS = (0,) + ORDER
KCH = 256
CHUNKS = 8


def mm(a, b):
    return jnp.dot(a, b, preferred_element_type=F32)


def mmt(a, b):
    return lax.dot_general(a, b, (((1,), (1,)), ((), ())), preferred_element_type=F32)


def eye(n):
    r = lax.broadcasted_iota(jnp.int32, (n, n), 0)
    c = lax.broadcasted_iota(jnp.int32, (n, n), 1)
    return jnp.where(r == c, 1.0, 0.0).astype(BF)


def lanes(i, n):
    return pl.ds(pl.multiple_of(i * n, n), n)


def up(n, m):
    return (n + m - 1) // m * m


def kernel(
    q_hbm, k_hbm, v_hbm, w_hbm, tgt_hbm, len_ref, seg_hbm,
    grad_rx, wg_ref, stat_ref,
    snd, w_ref, tgt_ref, rx, sib, segs, qt, kt, vt, km, vm, gk, gq, top_ref, s_ref, p_ref,
    ds_ref, w_tr, tgt_tr, attn_snd, attn_rx, go_snd, go_rx, gos, dq_acc, q_snd, xs_snd, xs_rx,
    own_kv, kv_snd,
    gt, gt_sib, attn_sib, stats, x_snd, x_rx, x_sum, z_snd, z_rx, y_snd, y_rx,
    lsem, ssem, rsem, rslot,
):
    x = lax.axis_index("dp_0")
    z = lax.axis_index("dp_1")
    y = lax.axis_index("patch_0")
    c = lax.axis_index("patch_1")
    nx = lax.axis_size("dp_0")
    nz = lax.axis_size("dp_1")
    HD = HEAD_DIM
    chip = lambda d: lax.rem(y + d, 8)
    at = lambda h: {"patch_0": h}
    back = lambda d: SLOTS.index((8 - d) % 8)
    xs = [(lax.rem(x + d, nx)) for d in range(1, nx)]
    zs = [(lax.rem(z + d, nz)) for d in range(1, nz)]
    sibling = {"patch_1": 1 - c}
    barrier = pltpu.get_barrier_semaphore()
    for d in range(1, 8):
        pl.semaphore_signal(barrier, inc=1, device_id=at(chip(d)), device_id_type=MESH)
    pl.semaphore_signal(barrier, inc=1, device_id=sibling, device_id_type=MESH)
    for o in xs:
        pl.semaphore_signal(barrier, inc=1, device_id={"dp_0": o}, device_id_type=MESH)
    for o in zs:
        pl.semaphore_signal(barrier, inc=1, device_id={"dp_1": o}, device_id_type=MESH)

    loads = [
        pltpu.make_async_copy(src, dst, lsem.at[i])
        for i, (src, dst) in enumerate((
            (q_hbm, snd.at[0]), (k_hbm, snd.at[1]), (v_hbm, snd.at[2]), (seg_hbm, segs.at[0, 0]),
            (w_hbm, w_ref), (tgt_hbm, tgt_ref)))
    ]
    for load in loads:
        load.start()

    def send(kind, src, dst, to, slot=None):
        return pltpu.make_async_remote_copy(
            src_ref=src, dst_ref=dst, send_sem=ssem.at[kind],
            recv_sem=rsem.at[kind] if slot is None else rslot.at[slot],
            device_id=to, device_id_type=MESH)

    for load in loads[:4]:
        load.wait()
    pl.semaphore_wait(barrier, 8 + len(xs) + len(zs))
    for d in ORDER:
        send(1, segs.at[0, 0], segs.at[0, back(d)], at(chip(d))).start()
    for d in ORDER:
        h = chip(d)
        send(0, snd.at[:, h], rx.at[back(d)], at(h), back(d)).start()
    send(2, snd.at[1:3, y], sib.at[0], sibling, 8).start()

    id256 = eye(256)
    id128 = eye(128)
    loads[4].wait()
    loads[5].wait()
    for j in range(5):
        n = 256 if j < 4 else 128
        cols = slice(256 * j, 256 * j + n)
        unit = id256 if n == 256 else id128
        w_tr[cols, :] = mmt(unit, w_ref[:, cols]).astype(BF)
        tgt_tr[cols, :] = mmt(unit, tgt_ref[:, cols]).astype(BF)
    length = len_ref[0]
    vt[HD:HD + 8, :] = jnp.ones((8, 16 * TOK), BF)
    top_ref[...] = jnp.full((8, 8 * TOK), NEG_LARGE, F32)

    def groups(parity, i):
        number = 2 * chip(SLOTS[i]) + (c if parity == 0 else 1 - c)
        at_pos = number * TOK + lax.broadcasted_iota(jnp.int32, (1, TOK), 1)
        group = jnp.where(at_pos < length, segs[parity, i], -1).astype(F32)
        row = (8 * parity + i) * TOK
        gk[row:row + TOK, :] = mmt(id128, jnp.broadcast_to(group, (TOK, TOK)).astype(BF))
        if parity == 0:
            gq[:, i * TOK:(i + 1) * TOK] = group

    def place(block, kb, vb):
        part = slice(block * TOK, (block + 1) * TOK)
        kt[:, part] = kb
        vt[0:HD, part] = vb
        km[part, :] = mmt(id128, kb).astype(BF)
        vm[part, :] = mmt(id128, vb).astype(BF)

    def running(v, op, into):
        for i in range(v.shape[0] // 8):
            into = op(into, v[8 * i:8 * i + 8])
        return into

    def score(block, q0, q1):
        part = slice(block * TOK, (block + 1) * TOK)
        sc = mm(km[part, :], qt[:, q0 * TOK:q1 * TOK])
        g = gk[part, :]
        for qb in range(q0, q1):
            cols = slice(qb * TOK, (qb + 1) * TOK)
            sub = jnp.where(g == gq[:, cols], sc[:, (qb - q0) * TOK:(qb - q0 + 1) * TOK], NEG_LARGE)
            s_ref[part, cols] = sub
            top_ref[:, cols] = running(sub, jnp.maximum, top_ref[:, cols])

    def place_own(i, qb, kb, vb):
        qt[:, i * TOK:(i + 1) * TOK] = qb
        place(i, kb, vb)
        if i:
            score(i, 0, i)
        for block in list(range(i + 1)) + [8 + j for j in range(i - 1)]:
            score(block, i, i + 1)

    def place_sibling(i, upto):
        send(2, rx.at[i, 1:3], sib.at[i], sibling, 8 + i).wait_recv()
        place(8 + i, sib[i, 0], sib[i, 1])
        for q0 in range(0, upto, 2):
            score(8 + i, q0, min(q0 + 2, upto))

    send(1, segs.at[0, 0:7], segs.at[0, 1:8], at(y)).wait_recv()
    send(3, segs.at[0], segs.at[1], sibling).start()
    for i in range(8):
        groups(0, i)
    place_own(0, snd[0, y], snd[1, y], snd[2, y])
    send(3, segs.at[0], segs.at[1], sibling).wait_recv()
    for i in range(8):
        groups(1, i)
    for i in range(1, 8):
        send(0, snd.at[:, y], rx.at[i], at(y), i).wait_recv()
        send(2, rx.at[i, 1:3], sib.at[i], sibling, 8 + i).start()
        place_own(i, rx[i, 0], rx[i, 1], rx[i, 2])
        place_sibling(i - 1, i + 1)
    place_sibling(7, 8)

    scale = 1.0 / math.sqrt(HEAD_DIM)
    to_two = scale / math.log(2.0)
    rdens = []
    for t in range(TILES):
        cols = slice(t * QTILE, (t + 1) * QTILE)
        top = jnp.max(top_ref[:, cols], axis=0, keepdims=True)
        for i in range(2 * CHUNKS):
            part = slice(i * TOK, (i + 1) * TOK)
            p_ref[part, cols] = jnp.exp2((s_ref[part, cols] - top) * to_two).astype(BF)
        sums = mm(vt[...], p_ref[:, cols])
        inv = 1.0 / sums[HD:HD + 1]
        rdens.append(inv)
        out = (sums[0:HD] * inv).astype(BF)
        for half in range(2):
            i = 2 * t + half
            attn_snd[i] = out[:, half * TOK:(half + 1) * TOK]
            if i:
                send(4, attn_snd.at[i], attn_rx.at[y], at(chip(SLOTS[i]))).start()

    attn_rx[y] = attn_snd[0]
    send(4, attn_snd.at[0:7], attn_rx.at[0:7], at(y)).wait_recv()

    send(10, attn_rx, attn_sib, sibling).start()
    attn_t = attn_rx[...].reshape(FEAT, TOK)
    position = (2 * y + c) * TOK + lax.broadcasted_iota(jnp.int32, (1, TOK), 1)
    live = position < length
    out_t = mm(w_tr[...], attn_t)
    error = jnp.where(live, out_t - tgt_tr[...].astype(F32), 0.0)
    grad_t = (2.0 * error).astype(BF)
    gt[...] = grad_t
    squares = running(error * error, jnp.add, jnp.zeros((8, TOK), F32))
    squares = jnp.sum(squares, axis=0, keepdims=True)
    lens = jnp.full((1, TOK), length.astype(F32), F32)
    row = lax.broadcasted_iota(jnp.int32, (8, TOK), 0)
    stats[0, 0] = jnp.where(row == 0, squares, jnp.where(row == 1, lens, 0.0))
    send(9, gt, gt_sib, sibling).start()
    send(11, stats.at[0, 0], stats.at[0, 1], sibling).start()
    go_snd[...] = mm(w_ref[...], grad_t).astype(BF).reshape(HEADS, HD, TOK)
    for d in ORDER:
        h = chip(d)
        send(5, go_snd.at[h], go_rx.at[back(d)], at(h)).start()
    go_rx[0] = go_snd[y]

    parts = []
    for h in range(HEADS):
        r = lax.broadcasted_iota(jnp.int32, (HALF_PAD, FEAT), 0)
        f = lax.broadcasted_iota(jnp.int32, (HALF_PAD, FEAT), 1)
        hit = jnp.logical_and(f - r == HD * h + HALF * c, r < HALF)
        parts.append(jnp.where(hit, 1.0, 0.0).astype(BF))
    pick = jnp.concatenate(parts, axis=0)
    send(10, attn_rx, attn_sib, sibling).wait_recv()
    attn_both = jnp.concatenate(
        [mm(pick, attn_t), mm(pick, attn_sib[...].reshape(FEAT, TOK))], axis=1).astype(BF)
    send(9, gt, gt_sib, sibling).wait_recv()
    send(11, stats.at[0, 0], stats.at[0, 1], sibling).wait_recv()
    stats[1, x] = stats[0, 0] + stats[0, 1]
    cx = WIDTH // nx
    cz = cx // nz
    czp = up(cz, 8)
    ch = cx // 2
    for half in range(2):
        for o in xs + [x]:
            rows = pl.ds(pl.multiple_of(o * cx + half * ch, 16), ch)
            both = jnp.concatenate([gt[rows, :], gt_sib[rows, :]], axis=1)
            x_snd[half, o] = mmt(both, attn_both).astype(BF)
            if o is not x:
                send(12 + half, x_snd.at[half, o], x_rx.at[half, x], {"dp_0": o}).start()
                if half == 0:
                    send(18, stats.at[1, x], stats.at[1, x], {"dp_0": o}).start()

    def sum_over_x(half):
        if nx > 1:
            send(12 + half, x_snd.at[half, 0:nx - 1], x_rx.at[half, 0:nx - 1], at(y)).wait_recv()
        acc = x_snd[half, x].astype(F32)
        for o in xs:
            acc = acc + x_rx[half, o].astype(F32)
        x_sum[half] = acc
        for k in range(nz // 2):
            to = half * (nz // 2) + k
            z_snd[to, 0:cz] = x_sum[half, k * cz:(k + 1) * cz, :].astype(BF)
            if czp > cz:
                z_snd[to, cz:czp] = jnp.zeros((czp - cz, LANES), BF)

            @pl.when(to != z)
            def _():
                send(14, z_snd.at[to], z_rx.at[z], {"dp_1": to}).start()

    send(5, go_snd.at[0:7], go_rx.at[1:8], at(y)).wait_recv()
    deltas = []
    for t in range(TILES):
        both = jnp.concatenate([go_rx[2 * t], go_rx[2 * t + 1]], axis=1).astype(F32)
        scaled = (both * rdens[t]).astype(BF)
        gos[:, t * QTILE:(t + 1) * QTILE] = scaled
        attn = jnp.concatenate([attn_snd[2 * t], attn_snd[2 * t + 1]], axis=1)
        deltas.append(jnp.sum(scaled.astype(F32) * attn.astype(F32), axis=0, keepdims=True))

    def backward(i, slot, first):
        part = slice(i * KCH, (i + 1) * KCH)
        for t in range(TILES):
            cols = slice(t * QTILE, (t + 1) * QTILE)
            dp = mm(vm[part, :], gos[:, cols])
            ds_ref[slot, :, cols] = (p_ref[part, cols].astype(F32) * (dp - deltas[t])).astype(BF)
        dv = mmt(gos[...], p_ref[part, :])
        dk = mmt(qt[...], ds_ref[slot]) * scale
        dq = mm(kt[:, part], ds_ref[slot])
        dq_acc[...] = dq if first else dq_acc[...] + dq
        return dk, dv

    def hand_over(j):
        send(7, xs_snd.at[j], xs_rx.at[j], sibling, 16 + j).wait_recv()
        for half in range(2):
            i = 2 * j + half
            cols = slice(half * TOK, (half + 1) * TOK)
            for g in range(2):
                kv_snd[g, i] = (own_kv[j, g, :, cols] + xs_rx[j, g, :, cols].astype(F32)).astype(BF)
            if i:
                send(8, kv_snd.at[:, i], grad_rx.at[1:3, y], at(chip(SLOTS[i]))).start()

    for j in range(4):
        dk, dv = backward(j + 4, 0, j == 0)
        xs_snd[j, 0] = dk.astype(BF)
        xs_snd[j, 1] = dv.astype(BF)
        send(7, xs_snd.at[j], xs_rx.at[j], sibling, 16 + j).start()
        dk, dv = backward(j, 1, False)
        own_kv[j, 0] = dk
        own_kv[j, 1] = dv
        if j:
            hand_over(j - 1)
    dq = (dq_acc[...] * scale).astype(BF)
    for i in range(8):
        q_snd[i] = dq[:, i * TOK:(i + 1) * TOK]
        if i:
            send(6, q_snd.at[i], grad_rx.at[0, y], at(chip(SLOTS[i]))).start()
    hand_over(3)
    grad_rx[0, y] = q_snd[0]
    grad_rx[1, y] = kv_snd[0, 0]
    grad_rx[2, y] = kv_snd[1, 0]

    sum_over_x(0)
    tot = stats[1, x]
    if nx > 1:
        send(18, stats.at[1, 0:nx - 1], stats.at[1, 0:nx - 1], at(y)).wait_recv()
    for o in xs:
        tot = tot + stats[1, o]
    stats[2, z] = tot
    for o in zs:
        send(15, stats.at[2, z], stats.at[2, z], {"dp_1": o}).start()
    sum_over_x(1)

    send(14, z_snd.at[0:nz - 1], z_rx.at[0:nz - 1], at(y)).wait_recv()
    send(15, stats.at[2, 0:nz - 1], stats.at[2, 0:nz - 1], at(y)).wait_recv()
    acc = z_snd[z].astype(F32)
    tot = stats[2, z]
    for o in zs:
        acc = acc + z_rx[o].astype(F32)
        tot = tot + stats[2, o]
    stats[3, y] = tot
    turned = mmt(eye(LANES), acc.astype(BF)).astype(BF)
    y_snd[:, :, 0:czp] = turned.reshape(HEADS, HALF_PAD, czp)
    for d in ORDER:
        h = chip(d)
        send(16, y_snd.at[h], y_rx.at[y], at(h)).start()
        send(17, stats.at[3, y], stats.at[3, y], at(h)).start()
    y_rx[y] = y_snd[y]
    send(6, q_snd.at[0:7], grad_rx.at[0, 0:7], at(y)).wait_recv()
    send(8, kv_snd.at[:, 0:7], grad_rx.at[1:3, 0:7], at(y)).wait_recv()
    send(16, y_snd.at[0:7], y_rx.at[0:7], at(y)).wait_recv()
    send(17, stats.at[3, 0:7], stats.at[3, 0:7], at(y)).wait_recv()
    tot = jnp.zeros((8, TOK), F32)
    acc = jnp.zeros((HALF_PAD, czp), F32)
    for s in range(8):
        tot = tot + stats[3, s]
        acc = acc + y_rx[s, :, 0:czp].astype(F32)
    stat_ref[...] = tot
    wg_ref[...] = acc[0:HALF, 0:cz]

    send(0, rx.at[0:7], rx.at[0:7], at(y), 0).wait_send()
    send(1, segs.at[0, 0:7], segs.at[0, 0:7], at(y)).wait_send()
    send(2, sib, sib, sibling, 8).wait_send()
    send(3, segs.at[0], segs.at[1], sibling).wait_send()
    send(4, attn_snd.at[0:7], attn_rx.at[0:7], at(y)).wait_send()
    send(5, go_snd.at[0:7], go_rx.at[1:8], at(y)).wait_send()
    send(6, q_snd.at[0:7], grad_rx.at[0, 0:7], at(y)).wait_send()
    send(7, xs_snd, xs_rx, sibling, 16).wait_send()
    send(8, kv_snd.at[:, 0:7], grad_rx.at[1:3, 0:7], at(y)).wait_send()
    send(9, gt, gt_sib, sibling).wait_send()
    send(10, attn_rx, attn_sib, sibling).wait_send()
    send(11, stats.at[0, 0], stats.at[0, 1], sibling).wait_send()
    if nx > 1:
        for half in range(2):
            send(12 + half, x_snd.at[half, 0:nx - 1], x_rx.at[half, 0:nx - 1], at(y)).wait_send()
        send(18, stats.at[1, 0:nx - 1], stats.at[1, 0:nx - 1], at(y)).wait_send()
    send(14, z_snd.at[0:nz - 1], z_rx.at[0:nz - 1], at(y)).wait_send()
    send(15, stats.at[2, 0:nz - 1], stats.at[2, 0:nz - 1], at(y)).wait_send()
    send(16, y_snd.at[0:7], y_rx.at[0:7], at(y)).wait_send()
    send(17, stats.at[3, 0:7], stats.at[3, 0:7], at(y)).wait_send()


def attention(q, k, v, w, target, lengths, segments):
    vm = pltpu.VMEM
    vmem = pl.BlockSpec(memory_space=pltpu.VMEM)
    hbm = pl.BlockSpec(memory_space=pltpu.HBM)
    keys = 16 * TOK
    nx = lax.axis_size("dp_0")
    nz = lax.axis_size("dp_1")
    cx = WIDTH // nx
    cz = cx // nz
    czp = up(cz, 8)
    HD = HEAD_DIM
    heads_of = lambda n: vm((HEADS, HD, TOK) if n is None else (HEADS, n, HD, TOK), BF)
    return pl.pallas_call(
        kernel,
        out_shape=[
            jax.ShapeDtypeStruct((3, HEADS, HD, TOK), BF),
            jax.ShapeDtypeStruct((HALF, cz), F32),
            jax.ShapeDtypeStruct((8, TOK), F32),
        ],
        in_specs=[hbm] * 5 + [pl.BlockSpec(memory_space=pltpu.SMEM), hbm],
        out_specs=[vmem] * 3,
        scratch_shapes=[
            vm((3, HEADS, HD, TOK), BF),
            vm((FEAT, WIDTH), BF),
            vm((TOK, WIDTH), BF),
            heads_of(3),
            heads_of(2),
            vm((2, HEADS, 1, TOK), jnp.int32),
            vm((HD, 8 * TOK), BF),
            vm((HD, keys), BF),
            vm((HD + 8, keys), BF),
            vm((keys, HD), BF),
            vm((keys, HD), BF),
            vm((keys, TOK), F32),
            vm((1, 8 * TOK), F32),
            vm((8, 8 * TOK), F32),
            vm((keys, 8 * TOK), F32),
            vm((keys, 8 * TOK), BF),
            vm((2, KCH, 8 * TOK), BF),
            vm((WIDTH, FEAT), BF),
            vm((WIDTH, TOK), BF),
            heads_of(None),
            heads_of(None),
            heads_of(None),
            heads_of(None),
            vm((HD, 8 * TOK), BF),
            vm((HD, 8 * TOK), F32),
            heads_of(None),
            vm((4, 2, HD, KCH), BF),
            vm((4, 2, HD, KCH), BF),
            vm((4, 2, HD, KCH), F32),
            vm((2, HEADS, HD, TOK), BF),
            vm((WIDTH, TOK), BF),
            vm((WIDTH, TOK), BF),
            heads_of(None),
            vm((4, 8, 8, TOK), F32),
            vm((2, nx, cx // 2, LANES), BF),
            vm((2, nx, cx // 2, LANES), BF),
            vm((2, cx // 2, LANES), F32),
            vm((nz, czp, LANES), BF),
            vm((nz, czp, LANES), BF),
            vm((HEADS, HALF_PAD, up(czp, 128)), BF),
            vm((HEADS, HALF_PAD, up(czp, 128)), BF),
            pltpu.SemaphoreType.DMA((6,)),
            pltpu.SemaphoreType.DMA((19,)),
            pltpu.SemaphoreType.DMA((19,)),
            pltpu.SemaphoreType.DMA((20,)),
        ],
        compiler_params=pltpu.CompilerParams(
            collective_id=0, has_side_effects=True, vmem_limit_bytes=40 * 1024 * 1024),
        name="attention",
    )(q, k, v, w, target, lengths, segments)


def finish(grads, part, stats, dq_ref, dk_ref, dv_ref, wg_ref, loss_ref):
    slots = 16 * TOK
    packs = lax.axis_size("dp_0") * lax.axis_size("dp_1")
    lens = stats[1:2]
    ratio = jnp.float32(slots * 16 * packs) / lens
    loss_ref[...] = jnp.sum(stats[0:1] / (lens * (WIDTH / 16)), axis=1, keepdims=True)
    wg_ref[...] = part[...] * (ratio[:, 0:1] * (1.0 / slots))
    for j, ref in enumerate((dq_ref, dk_ref, dv_ref)):
        ref[...] = grads[j].reshape(FEAT, TOK).astype(F32) * ratio


def local(query_rows, key_rows, value_rows, out_weight, target, lengths, segments):
    stay = lambda value: pltpu.with_memory_space_constraint(value, pltpu.HBM)
    by_head = lambda rows: stay(rows[0].T.reshape(HEADS, HEAD_DIM, TOK))
    grads, part, stats = attention(
        by_head(query_rows), by_head(key_rows), by_head(value_rows), stay(out_weight),
        stay(target[0]), lengths, stay(segments))
    vmem = pl.BlockSpec(memory_space=pltpu.VMEM)
    dq, dk, dv, weight, loss = pl.pallas_call(
        finish,
        out_shape=[jax.ShapeDtypeStruct((FEAT, TOK), F32)] * 3 + [
            jax.ShapeDtypeStruct(part.shape, F32), jax.ShapeDtypeStruct((1, 1), F32)],
        in_specs=[vmem] * 3,
        out_specs=[vmem] * 5,
        compiler_params=pltpu.CompilerParams(vmem_limit_bytes=8 * 1024 * 1024),
        name="finish",
    )(grads, part, stats)
    return (dq.T[None], dk.T[None], dv.T[None], weight, loss.reshape(()))


def solution(mesh):
    torus = Mesh(mesh.devices.reshape(4, 8, 8, 2), ("dp_0", "dp_1", "patch_0", "patch_1"))
    return jax.shard_map(
        local,
        mesh=torus,
        in_specs=(P(DP, PATCH, None), P(DP, PATCH, None), P(DP, PATCH, None), P(),
                  P(DP, PATCH, None), P(DP), P(DP, PATCH)),
        out_specs=(P(DP, PATCH, None), P(DP, PATCH, None), P(DP, PATCH, None), P(PATCH, DP), P()),
        check_vma=False,
    )
```

time: 68.1 us -> 65.3 us (0.959)
  Pallas kernels: 66.4 us -> 63.8 us
    pallas_call x1, Pallas kernels: 65.5 us -> 62.9 us  [attention(): pl.pallas_call(kernel, out_shape=[jax.ShapeDtypeStruct((3, HEADS, HD, TOK...]
where the time goes in v4:
time: 65.3 us; the launch traced here: 65.1 us
  Pallas kernels  63.8 us (98%)
  between operations  1.29 us (2%)
    pallas_call x1, Pallas kernels, attention(): pl.pallas_call(kernel, out_shape=[jax.ShapeDtypeStruct((3, HEADS, HD, TOK...  62.9 us

profile of v4, /device:TPU:1, one launch (start us, length us, event | category | flops | bytes accessed | tf_op | source)
XLA Modules:
  0.0 65.1 jit_solution(8324627117492539210)
XLA Ops:
  1.3 62.9 %attention.1 = (bf16[3,8,72,128]{3,2,1,0:T(8,128)(2,1)S(1)}, f32[36,36]{1,0:T(8,128)S(1)}, f32[8,128]{1,0:T(8,128)S(1)}) custom-call(bf16[8,72,128]{2,1,0:T(8,128)(2,1)} %bitcast.27, bf16[8,72,128]{2,1,0:T(8,128)(2,1)} %bitcast.28, bf16[8,72,128]{2,1,0:T(8,128)(2,1)} %bitcast.29, bf16[576,1152]{1,0:T(8,128)(2,1)} %w_hbm.1, bf16[128,1152]{1,0:T(8,128)(2,1)} %bitcast.26, ...), custom_call_target="tpu_custom_call" | custom-call | tf_op jit(solution)/shard_map/attention/pallas_call | solution.py:396
  64.2 0.9 %finish.1 = (f32[576,128]{1,0:T(8,128)}, f32[576,128]{1,0:T(8,128)}, f32[576,128]{1,0:T(8,128)}, f32[36,36]{1,0:T(8,128)}, f32[1,1]{1,0:T(1,128)}) custom-call(bf16[3,8,72,128]{3,2,1,0:T(8,128)(2,1)S(1)} %get-tuple-element.13.grads, f32[36,36]{1,0:T(8,128)S(1)} %get-tuple-element.14.part, f32[8,128]{1,0:T(8,128)S(1)} %get-tuple-element.15.stats), custom_call_target="tpu_custom_call" | custom-call | tf_op jit(solution)/shard_map/finish/pallas_call | solution.py:476
